TPU v7x, 256 devices: a whole 4x4x8 slice. The times are simulated.
256 devices in a mesh: sx: 16 (over y_hi, z), sy: 16 (over x, y_lo, core).
Axes of the slice: x: 4, y: 4 (y_hi: 2, y_lo: 2; y = y_hi * 2 + y_lo), z: 8, core: 2. Of those that a mesh axis runs over, the one named last changes fastest.
Arguments:
- tensors: bfloat16 [2, 16, 16, 1024, 256], P(None, 'sx', 'sy'), may hold values from -6 to 6
- gates: bfloat16 [8, 2, 2, 256, 256], replicated, may hold values from -0.1875 to 0.1875
- closing_rows: bfloat16 [2, 4096, 1024], P(None, ('sx', 'sy')), may hold values from -0.125 to 0.125
- closing_columns: float32 [2, 4096, 256], P(None, ('sx', 'sy')), may hold values from -0.25 to 0.25
Outputs:
- amplitudes: float32 [2, 4096], replicated
All inputs are finite; a program needn't handle non-finite values.
Results may differ from a plain program's by a relative error of at most 0.012.
Values may be sent and summed in bfloat16 or wider, within the bound.
A program may use at most 64 MiB of HBM per device.

v0:
```python
import jax
import jax.numpy as jnp
from jax import lax
from jax.sharding import PartitionSpec as P


def mixing_matrix(gate_pair, sign):
    own_top = jnp.concatenate([gate_pair[0, 0], gate_pair[0, 1]], axis=1)
    own_low = jnp.concatenate([-gate_pair[0, 1], gate_pair[0, 0]], axis=1)
    far_top = jnp.concatenate([gate_pair[1, 0], gate_pair[1, 1]], axis=1) * sign
    far_low = jnp.concatenate([-gate_pair[1, 1], gate_pair[1, 0]], axis=1) * sign
    return jnp.concatenate([own_top, own_low, far_top, far_low], axis=0)


def combine(own, partner, matrix):
    width = own.shape[-1]
    leading = own.shape[1:-1]
    joined = jnp.concatenate([own[0], own[1], partner[0], partner[1]], axis=-1).reshape(
        -1, 4 * width
    )
    result = jnp.dot(joined, matrix, preferred_element_type=jnp.float32).astype(jnp.bfloat16)
    real_part = result[:, :width].reshape(leading + (width,))
    imag_part = result[:, width:].reshape(leading + (width,))
    return jnp.stack([real_part, imag_part])


def local_section(grouped, gate_pair, axis_dim, bit_pos):
    shape = grouped.shape
    count = shape[axis_dim]
    split = shape[:axis_dim] + (count >> bit_pos + 1, 2, 1 << bit_pos) + shape[axis_dim + 1 :]
    blocks = grouped.reshape(split)
    lower = lax.index_in_dim(blocks, 0, axis_dim + 1, keepdims=False)
    upper = lax.index_in_dim(blocks, 1, axis_dim + 1, keepdims=False)
    new_lower = combine(lower, upper, mixing_matrix(gate_pair, 1.0))
    new_upper = combine(upper, lower, mixing_matrix(gate_pair, -1.0))
    return jnp.stack([new_lower, new_upper], axis=axis_dim + 1).reshape(shape)


def close_columns(projected, closing_columns):
    amp_real = jnp.sum(
        projected[0] * closing_columns[0] - projected[1] * closing_columns[1], axis=-1
    )
    amp_imag = jnp.sum(
        projected[0] * closing_columns[1] + projected[1] * closing_columns[0], axis=-1
    )
    return jnp.stack([amp_real, amp_imag])


def combine_rows(closing_rows, current):
    proj_real = jnp.dot(closing_rows[0], current[0], preferred_element_type=jnp.float32) - jnp.dot(
        closing_rows[1], current[1], preferred_element_type=jnp.float32
    )
    proj_imag = jnp.dot(closing_rows[0], current[1], preferred_element_type=jnp.float32) + jnp.dot(
        closing_rows[1], current[0], preferred_element_type=jnp.float32
    )
    return jnp.stack([proj_real, proj_imag])


def local(tensors, gates, closing_rows, closing_columns):
    current = tensors[:, 0, 0]
    rows_dev = current.shape[1]
    width = current.shape[2]
    count_x = lax.axis_size("sx")
    count_y = lax.axis_size("sy")
    bits_x = count_x.bit_length() - 1
    bits_y = count_y.bit_length() - 1
    grouped = lax.all_to_all(
        current.reshape(2, count_x, rows_dev // count_x, width),
        "sx",
        split_axis=1,
        concat_axis=1,
        tiled=True,
    )
    for bit_pos in range(bits_x):
        grouped = local_section(grouped, gates[bit_pos], 1, bit_pos)
    current = lax.all_to_all(grouped, "sx", split_axis=1, concat_axis=1, tiled=True).reshape(
        2, rows_dev, width
    )
    grouped = lax.all_to_all(
        current.reshape(2, count_y, rows_dev // count_y, width),
        "sy",
        split_axis=1,
        concat_axis=1,
        tiled=True,
    )
    for bit_pos in range(bits_y):
        grouped = local_section(grouped, gates[bits_x + bit_pos], 1, bit_pos)
    current = lax.all_to_all(grouped, "sy", split_axis=1, concat_axis=1, tiled=True).reshape(
        2, rows_dev, width
    )
    closed = close_columns(combine_rows(closing_rows, current), closing_columns)
    return lax.all_gather(closed, ("sx", "sy"), axis=1, tiled=True)


def solution(mesh):
    placed = (
        P(None, "sx", "sy", None, None),
        P(),
        P(None, ("sx", "sy"), None),
        P(None, ("sx", "sy"), None),
    )
    return jax.shard_map(local, mesh=mesh, in_specs=placed, out_specs=P(), check_vma=False)
```

profile of v0, /device:TPU:1, one launch (start us, length us, event | category | flops | bytes accessed | tf_op | source)
XLA Modules:
  0.0 485.2 jit_solution(15553791455334484417)
XLA Ops:
  0.0 2.3 copy.45
  2.3 11.7 %all-to-all-start = ((bf16[2,16,64,256]{3,2,0,1:T(8,128)(2,1)}), bf16[2,16,64,256]{3,2,0,1:T(8,128)(2,1)S(1)}, u32[]{:S(2)}, u32[]{:S(2)}) async-start(bf16[2,16,64,256]{3,2,0,1:T(8,128)(2,1)} %copy.45), calls=%async_computation | async-start | bytes 2097152 | tf_op jit(solution)/shard_map/all_to_all | solution.py:67
  14.1 2.5 slice_bitcast_fusion
  16.5 0.8 fusion.240
  17.3 0.9 slice_bitcast_fusion.34
  18.2 1.0 maximum_multiply_fusion
  19.2 0.9 maximum_multiply_fusion.2
  20.1 0.7 fusion.244
  20.8 0.9 slice_bitcast_fusion.26
  21.8 0.9 maximum_multiply_fusion.4
  22.7 0.9 maximum_multiply_fusion.6
  23.6 17.5 %all-to-all-done = bf16[2,16,64,256]{3,2,0,1:T(8,128)(2,1)S(1)} async-done(((bf16[2,16,64,256]{3,2,0,1:T(8,128)(2,1)}), bf16[2,16,64,256]{3,2,0,1:T(8,128)(2,1)S(1)}, u32[]{:S(2)}, u32[]{:S(2)}) %all-to-all-start) | async-done | bytes 1048608 | tf_op jit(solution)/shard_map/all_to_all | solution.py:67
  41.2 0.8 copy-done.8
  42.3 0.7 convolution_convert_fusion.15
  43.0 0.2 copy-done.36
  43.3 0.7 convolution_convert_fusion.14
  44.5 0.7 copy-done.3
  45.5 0.7 convolution_convert_fusion.13
  46.2 0.2 copy-done.32
  46.5 0.7 convolution_convert_fusion.12
  47.5 0.1 pad_maximum_fusion
  47.6 0.7 copy-done.1
  48.6 0.7 convolution_convert_fusion.11
  49.3 0.2 copy-done.28
  49.6 0.7 convolution_convert_fusion.10
  50.6 0.1 pad_maximum_fusion.1
  50.8 0.7 copy-done.12
  51.6 0.7 convolution_convert_fusion.9
  52.4 0.2 copy-done.26
  52.7 0.7 convolution_convert_fusion.8
  53.7 1.1 copy.54
  54.8 6.2 %all-to-all-start.1 = ((bf16[2,16,64,256]{3,2,0,1:T(8,128)(2,1)}), bf16[2,16,64,256]{3,2,0,1:T(8,128)(2,1)}, u32[]{:S(2)}, u32[]{:S(2)}) async-start(bf16[2,16,64,256]{3,2,0,1:T(8,128)(2,1)} %copy.54), calls=%async_computation.1 | async-start | bytes 2097152 | tf_op jit(solution)/shard_map/all_to_all | solution.py:76
  60.9 0.8 fusion.248
  61.7 0.9 slice_bitcast_fusion.18
  62.6 25.4 %all-to-all-done.1 = bf16[2,16,64,256]{3,2,0,1:T(8,128)(2,1)} async-done(((bf16[2,16,64,256]{3,2,0,1:T(8,128)(2,1)}), bf16[2,16,64,256]{3,2,0,1:T(8,128)(2,1)}, u32[]{:S(2)}, u32[]{:S(2)}) %all-to-all-start.1) | async-done | bytes 1048608 | tf_op jit(solution)/shard_map/all_to_all | solution.py:76
  88.0 7.0 %all-to-all-start.2 = ((bf16[2,16,64,256]{3,2,0,1:T(8,128)(2,1)}), bf16[2,16,64,256]{3,2,0,1:T(8,128)(2,1)S(1)}, u32[]{:S(2)}, u32[]{:S(2)}) async-start(bf16[2,16,64,256]{3,2,0,1:T(8,128)(2,1)} %all-to-all-done.1), calls=%async_computation.2 | async-start | bytes 2097152 | tf_op jit(solution)/shard_map/all_to_all | solution.py:79
  95.0 0.9 maximum_multiply_fusion.8
  95.9 0.9 maximum_multiply_fusion.10
  96.8 0.7 fusion.252
  97.6 0.9 slice_bitcast_fusion.10
  98.7 11.8 %all-to-all-done.2 = bf16[2,16,64,256]{3,2,0,1:T(8,128)(2,1)S(1)} async-done(((bf16[2,16,64,256]{3,2,0,1:T(8,128)(2,1)}), bf16[2,16,64,256]{3,2,0,1:T(8,128)(2,1)S(1)}, u32[]{:S(2)}, u32[]{:S(2)}) %all-to-all-start.2) | async-done | bytes 1048608 | tf_op jit(solution)/shard_map/all_to_all | solution.py:79
  110.5 0.8 copy-done.51
  111.5 0.7 convolution_convert_fusion.7
  112.2 0.2 copy-done.34
  112.5 0.7 convolution_convert_fusion.6
  113.6 0.7 copy-done.20
  114.5 0.7 convolution_convert_fusion.5
  115.2 0.2 copy-done.30
  115.5 0.7 convolution_convert_fusion.4
  116.5 0.1 pad_maximum_fusion.3
  116.7 0.7 copy-done.18
  117.6 0.7 convolution_convert_fusion.3
  118.3 0.7 convolution_convert_fusion.2
  119.2 0.1 pad_maximum_fusion.4
  119.4 0.7 copy-done.14
  120.3 0.7 convolution_convert_fusion.1
  121.0 0.7 convolution_convert_fusion
  122.2 19.4 %all_to_all.20 = bf16[2,16,64,256]{3,2,0,1:T(8,128)(2,1)S(1)} all-to-all(bf16[2,16,64,256]{3,2,0,1:T(8,128)(2,1)S(1)} %copy.63), channel_id=1, replica_groups=mesh['sx'=16,'sy'=16] {'sy'}, dimensions={1} | all-to-all | bytes 2097152 | tf_op jit(solution)/shard_map/all_to_all | solution.py:88
  141.6 0.2 fusion.212
  141.8 0.2 fusion.214
  142.0 0.2 fusion.1
  142.3 0.3 fusion.221
  142.6 341.8 %all-gather = f32[256,16,2]{1,2,0:T(2,128)S(1)} all-gather(f32[1,16,2]{1,2,0:T(2,128)S(1)} %maximum_bitcast_fusion.12), channel_id=1, replica_groups=mesh['sx'=16,'sy'=16] {'sx','sy'}, dimensions={0}, use_global_device_ids=true | all-gather | bytes 32896 | tf_op jit(solution)/shard_map/all_gather | solution.py:92
  484.4 0.8 reshape.254
  (168 shorter events, 5.2 us)
Async XLA Ops:
  2.3 38.8 %all-to-all-start = ((bf16[2,16,64,256]{3,2,0,1:T(8,128)(2,1)}), bf16[2,16,64,256]{3,2,0,1:T(8,128)(2,1)S(1)}, u32[]{:S(2)}, u32[]{:S(2)}) async-start(bf16[2,16,64,256]{3,2,0,1:T(8,128)(2,1)} %copy.45), calls=%async_computation | async-start | bytes 2097152 | tf_op jit(solution)/shard_map/all_to_all | solution.py:67
  17.3 2.8 copy-start.21
  17.3 2.8 copy-start.24
  18.2 1.9 copy-start.2
  18.2 3.5 copy-start.4
  18.2 3.5 copy-start.7
  18.2 3.5 copy-start.9
  20.8 1.8 copy-start.11
  20.8 1.8 copy-start.15
  41.1 1.0 copy-start.10
  41.1 1.0 copy-start.25
  41.1 1.1 copy-start.53
  41.1 1.2 copy-start.54
  41.1 1.2 copy-start.62
  42.3 0.9 copy-start.36
  42.3 1.0 copy-start.37
  44.2 0.9 copy-start.3
  44.3 1.0 copy-start.5
  44.3 1.0 copy-start.22
  44.3 1.1 copy-start.49
  44.3 1.1 copy-start.50
  44.3 1.2 copy-start.60
  45.5 0.9 copy-start.32
  45.5 1.0 copy-start.33
  47.4 0.9 copy-start.1
  47.4 1.0 copy-start.16
  47.4 1.0 copy-start.43
  47.4 1.1 copy-start.44
  47.5 1.1 copy-start.57
  48.6 0.9 copy-start.28
  48.6 1.0 copy-start.29
  50.5 0.9 copy-start.12
  50.5 1.0 copy-start.39
  50.6 1.0 copy-start.40
  50.6 1.1 copy-start.55
  51.6 0.9 copy-start.26
  51.6 1.0 copy-start.27
  54.8 33.3 %all-to-all-start.1 = ((bf16[2,16,64,256]{3,2,0,1:T(8,128)(2,1)}), bf16[2,16,64,256]{3,2,0,1:T(8,128)(2,1)}, u32[]{:S(2)}, u32[]{:S(2)}) async-start(bf16[2,16,64,256]{3,2,0,1:T(8,128)(2,1)} %copy.54), calls=%async_computation.1 | async-start | bytes 2097152 | tf_op jit(solution)/shard_map/all_to_all | solution.py:76
  62.6 32.4 %copy-start.6 = (bf16[256,256]{1,0:T(8,128)(2,1)S(1)}, bf16[256,256]{1,0:T(8,128)(2,1)}, u32[]{:S(2)}) copy-start(bf16[256,256]{1,0:T(8,128)(2,1)} %get-tuple-element.151) | copy-start | bytes 393220
  62.6 32.4 %copy-start.23 = (bf16[256,256]{1,0:T(8,128)(2,1)S(1)}, bf16[256,256]{1,0:T(8,128)(2,1)}, u32[]{:S(2)}) copy-start(bf16[256,256]{1,0:T(8,128)(2,1)} %get-tuple-element.88) | copy-start | bytes 393220
  62.6 33.3 %copy-start.19 = (bf16[256,256]{1,0:T(8,128)(2,1)S(1)}, bf16[256,256]{1,0:T(8,128)(2,1)}, u32[]{:S(2)}) copy-start(bf16[256,256]{1,0:T(8,128)(2,1)} %get-tuple-element.165) | copy-start | bytes 393220
  88.0 22.4 %all-to-all-start.2 = ((bf16[2,16,64,256]{3,2,0,1:T(8,128)(2,1)}), bf16[2,16,64,256]{3,2,0,1:T(8,128)(2,1)S(1)}, u32[]{:S(2)}, u32[]{:S(2)}) async-start(bf16[2,16,64,256]{3,2,0,1:T(8,128)(2,1)} %all-to-all-done.1), calls=%async_computation.2 | async-start | bytes 2097152 | tf_op jit(solution)/shard_map/all_to_all | solution.py:79
  97.6 13.0 %copy-start.13 = (bf16[256,256]{1,0:T(8,128)(2,1)}, bf16[256,256]{1,0:T(8,128)(2,1)S(1)}, u32[]{:S(2)}) copy-start(bf16[256,256]{1,0:T(8,128)(2,1)S(1)} %get-tuple-element.167) | copy-start | bytes 393220
  97.6 13.0 %copy-start.17 = (bf16[256,256]{1,0:T(8,128)(2,1)}, bf16[256,256]{1,0:T(8,128)(2,1)S(1)}, u32[]{:S(2)}) copy-start(bf16[256,256]{1,0:T(8,128)(2,1)S(1)} %get-tuple-element.68) | copy-start | bytes 393220
  110.4 0.9 copy-start.51
  110.4 1.0 copy-start.52
  110.4 1.0 copy-start.61
  111.5 0.9 copy-start.34
  111.5 1.0 copy-start.35
  113.4 0.9 copy-start.20
  113.4 1.0 copy-start.47
  113.4 1.0 copy-start.48
  113.4 1.1 copy-start.59
  114.5 0.9 copy-start.30
  114.5 1.0 copy-start.31
  116.5 0.9 copy-start.18
  116.5 1.0 copy-start.45
  116.5 1.0 copy-start.46
  116.5 1.1 copy-start.58
  119.2 0.9 copy-start.14
  119.2 1.0 copy-start.41
  119.2 1.0 copy-start.42
  119.2 1.1 copy-start.56
  122.2 19.5 %copy-start.38 = (bf16[2,16,1024]{2,1,0:T(8,128)(2,1)S(1)}, bf16[2,16,1024]{2,1,0:T(8,128)(2,1)}, u32[]{:S(2)}) copy-start(bf16[2,16,1024]{2,1,0:T(8,128)(2,1)} %param.6) | copy-start | bytes 196612
  (3 other events, 2.6 us)
where the time goes:
time: 486 us; the launch traced here: 485 us
  blocking collectives  361 us (74%)
  waiting for transfers between devices  54.8 us (11%)
  starting transfers between devices  24.8 us (5%)
  local copies, waits for them, and re-layouts  21.2 us (4%)
  matrix products  12.2 us (3%)
  other arithmetic  10.1 us (2%)
    all_gather x1, blocking collectives, local(): return lax.all_gather(closed, ('sx', 'sy'), axis=1, tiled=True)  342 us
    all_to_all x1, waiting for transfers between devices, local(): lax.all_to_all(grouped, 'sx', split_axis=1, concat_axis=1, tiled=True)  25.4 us
    all_to_all x1, blocking collectives, local(): lax.all_to_all(grouped, 'sy', split_axis=1, concat_axis=1, tiled=True)  19.4 us
    all_to_all x1, waiting for transfers between devices, local(): lax.all_to_all(current.reshape(2, count_x, rows_dev // count_x, width), '...  17.5 us
    all_to_all x1, waiting for transfers between devices, local(): lax.all_to_all(current.reshape(2, count_y, rows_dev // count_y, width), '...  11.8 us
    all_to_all x1, starting transfers between devices, local(): lax.all_to_all(current.reshape(2, count_x, rows_dev // count_x, width), '...  11.7 us
    dot_general x16, matrix products, combine(): jnp.dot(joined, matrix, preferred_element_type=jnp.float32)  11.3 us
    unnamed x137, local copies, waits for them, and re-layouts  10.4 us
  transfers between devices with their start and end apart: 3, of which 3 were waited for; matrix products, arithmetic and copies ran while one was open for 3% of the time, Pallas kernels for 0%

commit v1 on v0

--- a/solution.py
+++ b/solution.py
@@ -1,7 +1,76 @@
+import functools
+
 import jax
 import jax.numpy as jnp
 from jax import lax
+from jax.experimental import pallas as pl
+from jax.experimental.pallas import tpu as pltpu
 from jax.sharding import PartitionSpec as P
+
+MESH = pl.DeviceIdType.MESH
+
+
+def gather_kernel(count_x, count_y, own_ref, out_ref, send_x, recv_x, send_y, recv_y):
+    sx = lax.axis_index("sx")
+    sy = lax.axis_index("sy")
+    barrier = pltpu.get_barrier_semaphore()
+    for step in range(1, count_x):
+        peer = lax.rem(sx + step, count_x)
+        pl.semaphore_signal(barrier, inc=1, device_id=(peer, sy), device_id_type=MESH)
+    for step in range(1, count_y):
+        peer = lax.rem(sy + step, count_y)
+        pl.semaphore_signal(barrier, inc=1, device_id=(sx, peer), device_id_type=MESH)
+    pl.semaphore_wait(barrier, count_x + count_y - 2)
+    copies = []
+    for step in range(1, count_x):
+        copy = pltpu.make_async_remote_copy(
+            src_ref=own_ref,
+            dst_ref=out_ref.at[sy, sx],
+            send_sem=send_x.at[step - 1],
+            recv_sem=recv_x.at[step - 1],
+            device_id=(lax.rem(sx + step, count_x), sy),
+            device_id_type=MESH,
+        )
+        copy.start()
+        copies.append(copy)
+    out_ref[sy, sx] = own_ref[...]
+    for copy in copies:
+        copy.wait()
+    copies = []
+    for step in range(1, count_y):
+        copy = pltpu.make_async_remote_copy(
+            src_ref=out_ref.at[sy],
+            dst_ref=out_ref.at[sy],
+            send_sem=send_y.at[step - 1],
+            recv_sem=recv_y.at[step - 1],
+            device_id=(sx, lax.rem(sy + step, count_y)),
+            device_id_type=MESH,
+        )
+        copy.start()
+        copies.append(copy)
+    for copy in copies:
+        copy.wait()
+
+
+def gather_amplitudes(closed, count_x, count_y):
+    amps = closed.shape[1]
+    row = jnp.concatenate([closed.reshape(1, 2 * amps), jnp.zeros((1, 128 - 2 * amps), jnp.float32)], axis=1)
+    rows = pl.pallas_call(
+        functools.partial(gather_kernel, count_x, count_y),
+        out_shape=jax.ShapeDtypeStruct((count_y, count_x, 1, 128), jnp.float32),
+        in_specs=[pl.BlockSpec(memory_space=pltpu.VMEM)],
+        out_specs=pl.BlockSpec(memory_space=pltpu.VMEM),
+        scratch_shapes=[
+            pltpu.SemaphoreType.DMA((count_x - 1,)),
+            pltpu.SemaphoreType.DMA((count_x - 1,)),
+            pltpu.SemaphoreType.DMA((count_y - 1,)),
+            pltpu.SemaphoreType.DMA((count_y - 1,)),
+        ],
+        compiler_params=pltpu.CompilerParams(collective_id=0, has_side_effects=True),
+        name="gather",
+    )(row)
+    rows = rows[:, :, 0, : 2 * amps].reshape(count_y, count_x, 2, amps)
+    return rows.transpose(2, 1, 0, 3).reshape(2, count_x * count_y * amps)
 
 
 def mixing_matrix(gate_pair, sign):
@@ -89,7 +158,7 @@
         2, rows_dev, width
     )
     closed = close_columns(combine_rows(closing_rows, current), closing_columns)
-    return lax.all_gather(closed, ("sx", "sy"), axis=1, tiled=True)
+    return gather_amplitudes(closed, count_x, count_y)
 
 
 def solution(mesh):

time: 486 us -> 162 us (0.33)
  blocking collectives: 361 us -> 19.4 us
  Pallas kernels: 0 us -> 15.7 us
    all_gather x1 -> x0, blocking collectives: 342 us -> none  [local(): return lax.all_gather(closed, ('sx', 'sy'), axis=1, tiled=True)]
    pallas_call x0 -> x1, Pallas kernels: none -> 15.7 us  [gather_amplitudes(): pl.pallas_call(functools.partial(gather_kernel, count_x, count_y), out_sh...]
    unnamed x137 -> x150, local copies, waits for them, and re-layouts: 10.4 us -> 9.44 us
  transfers between devices with their start and end apart: 3 -> 3, of which waited for: 3 -> 3; matrix products, arithmetic and copies ran while one was open for 3% -> 10% of each run, Pallas kernels for 0% -> 0%
where the time goes in v1:
time: 162 us; the launch traced here: 161 us
  waiting for transfers between devices  53.1 us (33%)
  starting transfers between devices  24.8 us (15%)
  local copies, waits for them, and re-layouts  23.2 us (14%)
  blocking collectives  19.4 us (12%)
  Pallas kernels  15.7 us (10%)
  matrix products  12.2 us (8%)
  other arithmetic  11.7 us (7%)
    all_to_all x1, waiting for transfers between devices, local(): lax.all_to_all(grouped, 'sx', split_axis=1, concat_axis=1, tiled=True)  25.4 us
    all_to_all x1, blocking collectives, local(): lax.all_to_all(grouped, 'sy', split_axis=1, concat_axis=1, tiled=True)  19.4 us
    all_to_all x1, waiting for transfers between devices, local(): lax.all_to_all(current.reshape(2, count_x, rows_dev // count_x, width), '...  17.5 us
    pallas_call x1, Pallas kernels, gather_amplitudes(): pl.pallas_call(functools.partial(gather_kernel, count_x, count_y), out_sh...  15.7 us
    all_to_all x1, starting transfers between devices, local(): lax.all_to_all(current.reshape(2, count_x, rows_dev // count_x, width), '...  11.7 us
    dot_general x16, matrix products, combine(): jnp.dot(joined, matrix, preferred_element_type=jnp.float32)  11.3 us
    all_to_all x1, waiting for transfers between devices, local(): lax.all_to_all(current.reshape(2, count_y, rows_dev // count_y, width), '...  10.2 us
    unnamed x150, local copies, waits for them, and re-layouts  9.44 us
  transfers between devices with their start and end apart: 3, of which 3 were waited for; matrix products, arithmetic and copies ran while one was open for 10% of the time, Pallas kernels for 0%

profile of v1, /device:TPU:1, one launch (start us, length us, event | category | flops | bytes accessed | tf_op | source)
XLA Modules:
  0.0 161.1 jit_solution(919073224971297553)
XLA Ops:
  0.0 2.3 %copy.46 = bf16[2,16,64,256]{3,2,0,1:T(8,128)(2,1)} copy(bf16[2,16,64,256]{3,2,1,0:T(8,128)(2,1)} %bitcast.282) | data formatting | bytes 2097152 | tf_op jit(solution)/shard_map/reshape;squeeze | solution.py:137
  2.3 11.7 %all-to-all-start = ((bf16[2,16,64,256]{3,2,0,1:T(8,128)(2,1)}), bf16[2,16,64,256]{3,2,0,1:T(8,128)(2,1)S(1)}, u32[]{:S(2)}, u32[]{:S(2)}) async-start(bf16[2,16,64,256]{3,2,0,1:T(8,128)(2,1)} %copy.46), calls=%async_computation | async-start | bytes 2097152 | tf_op jit(solution)/shard_map/all_to_all | solution.py:136
  14.1 2.5 %slice_bitcast_fusion = (bf16[2,2,256,256]{3,2,1,0:T(8,128)(2,1)S(1)}, bf16[2,2,256,256]{3,2,1,0:T(8,128)(2,1)S(1)}, bf16[2,2,256,256]{3,2,1,0:T(8,128)(2,1)S(1)...) fusion(bf16[8,2,2,256,256]{4,3,2,1,0:T(8,128)(2,1)} %param.5), kind=kLoop, calls=%fused_computation.256 | loop fusion | bytes 8388608 | tf_op jit(solution)/shard_map/squeeze | solution.py:156
  16.6 0.8 fusion.240
  17.4 0.9 slice_bitcast_fusion.34
  18.3 1.0 maximum_multiply_fusion
  19.2 0.9 maximum_multiply_fusion.2
  20.1 0.8 fusion.244
  20.9 0.9 slice_bitcast_fusion.26
  21.8 0.9 maximum_multiply_fusion.4
  22.7 0.9 maximum_multiply_fusion.6
  23.6 17.5 %all-to-all-done = bf16[2,16,64,256]{3,2,0,1:T(8,128)(2,1)S(1)} async-done(((bf16[2,16,64,256]{3,2,0,1:T(8,128)(2,1)}), bf16[2,16,64,256]{3,2,0,1:T(8,128)(2,1)S(1)}, u32[]{:S(2)}, u32[]{:S(2)}) %all-to-all-start) | async-done | bytes 1048608 | tf_op jit(solution)/shard_map/all_to_all | solution.py:136
  41.2 0.8 copy-done.8
  42.3 0.7 convolution_convert_fusion.15
  43.0 0.2 copy-done.40
  43.4 0.7 convolution_convert_fusion.14
  44.5 0.7 copy-done.3
  45.5 0.7 convolution_convert_fusion.13
  46.2 0.2 copy-done.36
  46.5 0.7 convolution_convert_fusion.12
  47.7 0.7 copy-done.1
  48.6 0.7 convolution_convert_fusion.11
  49.3 0.2 copy-done.30
  49.6 0.7 convolution_convert_fusion.10
  50.8 0.7 copy-done.12
  51.7 0.7 convolution_convert_fusion.9
  52.4 0.2 copy-done.26
  52.7 0.7 convolution_convert_fusion.8
  53.7 1.0 copy.55
  54.7 6.2 %all-to-all-start.1 = ((bf16[2,16,64,256]{3,2,0,1:T(8,128)(2,1)}), bf16[2,16,64,256]{3,2,0,1:T(8,128)(2,1)}, u32[]{:S(2)}, u32[]{:S(2)}) async-start(bf16[2,16,64,256]{3,2,0,1:T(8,128)(2,1)} %copy.55), calls=%async_computation.1 | async-start | bytes 2097152 | tf_op jit(solution)/shard_map/all_to_all | solution.py:145
  60.9 0.8 fusion.248
  61.7 0.9 slice_bitcast_fusion.18
  62.6 25.4 %all-to-all-done.1 = bf16[2,16,64,256]{3,2,0,1:T(8,128)(2,1)} async-done(((bf16[2,16,64,256]{3,2,0,1:T(8,128)(2,1)}), bf16[2,16,64,256]{3,2,0,1:T(8,128)(2,1)}, u32[]{:S(2)}, u32[]{:S(2)}) %all-to-all-start.1) | async-done | bytes 1048608 | tf_op jit(solution)/shard_map/all_to_all | solution.py:145
  88.0 7.0 %all-to-all-start.2 = ((bf16[2,16,64,256]{3,2,0,1:T(8,128)(2,1)}), bf16[2,16,64,256]{3,2,0,1:T(8,128)(2,1)S(1)}, u32[]{:S(2)}, u32[]{:S(2)}) async-start(bf16[2,16,64,256]{3,2,0,1:T(8,128)(2,1)} %all-to-all-done.1), calls=%async_computation.2 | async-start | bytes 2097152 | tf_op jit(solution)/shard_map/all_to_all | solution.py:148
  95.0 0.9 maximum_multiply_fusion.8
  95.9 0.9 maximum_multiply_fusion.10
  96.8 0.7 fusion.252
  97.5 0.9 slice_bitcast_fusion.10
  98.4 0.9 maximum_multiply_fusion.12
  99.3 0.9 maximum_multiply_fusion.14
  100.2 10.2 %all-to-all-done.2 = bf16[2,16,64,256]{3,2,0,1:T(8,128)(2,1)S(1)} async-done(((bf16[2,16,64,256]{3,2,0,1:T(8,128)(2,1)}), bf16[2,16,64,256]{3,2,0,1:T(8,128)(2,1)S(1)}, u32[]{:S(2)}, u32[]{:S(2)}) %all-to-all-start.2) | async-done | bytes 1048608 | tf_op jit(solution)/shard_map/all_to_all | solution.py:148
  110.6 0.7 convolution_convert_fusion.7
  111.7 0.7 convolution_convert_fusion.6
  112.8 0.7 copy-done.20
  113.7 0.7 convolution_convert_fusion.5
  114.4 0.2 copy-done.34
  114.7 0.7 convolution_convert_fusion.4
  115.9 0.7 copy-done.18
  116.8 0.7 convolution_convert_fusion.3
  117.5 0.2 copy-done.32
  117.8 0.7 convolution_convert_fusion.2
  118.9 0.7 copy-done.14
  119.8 0.7 convolution_convert_fusion.1
  120.5 0.2 copy-done.28
  120.8 0.7 convolution_convert_fusion
  121.9 19.4 %all_to_all.20 = bf16[2,16,64,256]{3,2,0,1:T(8,128)(2,1)S(1)} all-to-all(bf16[2,16,64,256]{3,2,0,1:T(8,128)(2,1)S(1)} %copy.64), channel_id=1, replica_groups=mesh['sx'=16,'sy'=16] {'sy'}, dimensions={1} | all-to-all | bytes 2097152 | tf_op jit(solution)/shard_map/all_to_all | solution.py:157
  141.6 0.2 fusion.214
  141.8 0.2 fusion.1
  142.1 0.3 fusion.221
  142.5 0.5 concatenate.409.own_ref
  143.0 15.7 %gather.1 = f32[16,16,1,128]{3,2,1,0:T(1,128)} custom-call(f32[1,128]{1,0:T(1,128)} %concatenate.409.own_ref), custom_call_target="tpu_custom_call" | custom-call | tf_op jit(solution)/shard_map/gather/pallas_call | solution.py:58
  158.7 1.3 slice_reduce_fusion
  160.0 0.2 reshape_squeeze.7
  160.3 0.8 reshape.260
  (186 shorter events, 6.1 us)
Async XLA Ops:
  2.3 38.8 %all-to-all-start = ((bf16[2,16,64,256]{3,2,0,1:T(8,128)(2,1)}), bf16[2,16,64,256]{3,2,0,1:T(8,128)(2,1)S(1)}, u32[]{:S(2)}, u32[]{:S(2)}) async-start(bf16[2,16,64,256]{3,2,0,1:T(8,128)(2,1)} %copy.46), calls=%async_computation | async-start | bytes 2097152 | tf_op jit(solution)/shard_map/all_to_all | solution.py:136
  17.4 2.8 %copy-start.21 = (bf16[256,256]{1,0:T(8,128)(2,1)}, bf16[256,256]{1,0:T(8,128)(2,1)S(1)}, u32[]{:S(2)}) copy-start(bf16[256,256]{1,0:T(8,128)(2,1)S(1)} %get-tuple-element.161) | copy-start | bytes 393220
  17.4 2.8 %copy-start.24 = (bf16[256,256]{1,0:T(8,128)(2,1)}, bf16[256,256]{1,0:T(8,128)(2,1)S(1)}, u32[]{:S(2)}) copy-start(bf16[256,256]{1,0:T(8,128)(2,1)S(1)} %get-tuple-element.128) | copy-start | bytes 393220
  18.3 1.9 %copy-start.2 = (bf16[256,256]{1,0:T(8,128)(2,1)}, bf16[256,256]{1,0:T(8,128)(2,1)S(1)}, u32[]{:S(2)}) copy-start(bf16[256,256]{1,0:T(8,128)(2,1)S(1)} %get-tuple-element.114) | copy-start | bytes 393220
  18.3 3.5 %copy-start.4 = (bf16[256,256]{1,0:T(8,128)(2,1)}, bf16[256,256]{1,0:T(8,128)(2,1)S(1)}, u32[]{:S(2)}) copy-start(bf16[256,256]{1,0:T(8,128)(2,1)S(1)} %get-tuple-element.115) | copy-start | bytes 393220
  18.3 3.5 %copy-start.7 = (bf16[256,256]{1,0:T(8,128)(2,1)}, bf16[256,256]{1,0:T(8,128)(2,1)S(1)}, u32[]{:S(2)}) copy-start(bf16[256,256]{1,0:T(8,128)(2,1)S(1)} %get-tuple-element.158) | copy-start | bytes 393220
  18.3 3.5 %copy-start.9 = (bf16[256,256]{1,0:T(8,128)(2,1)}, bf16[256,256]{1,0:T(8,128)(2,1)S(1)}, u32[]{:S(2)}) copy-start(bf16[256,256]{1,0:T(8,128)(2,1)S(1)} %get-tuple-element.159) | copy-start | bytes 393220
  20.9 1.8 %copy-start.11 = (bf16[256,256]{1,0:T(8,128)(2,1)}, bf16[256,256]{1,0:T(8,128)(2,1)S(1)}, u32[]{:S(2)}) copy-start(bf16[256,256]{1,0:T(8,128)(2,1)S(1)} %get-tuple-element.163) | copy-start | bytes 393220
  20.9 1.8 %copy-start.15 = (bf16[256,256]{1,0:T(8,128)(2,1)}, bf16[256,256]{1,0:T(8,128)(2,1)S(1)}, u32[]{:S(2)}) copy-start(bf16[256,256]{1,0:T(8,128)(2,1)S(1)} %get-tuple-element.108) | copy-start | bytes 393220
  41.1 1.0 copy-start.10
  41.1 1.0 copy-start.25
  41.1 1.1 copy-start.59
  41.1 1.2 copy-start.60
  41.1 1.2 copy-start.69
  42.3 0.9 copy-start.40
  42.3 1.0 copy-start.41
  44.3 1.0 copy-start.5
  44.3 1.0 copy-start.22
  44.3 1.1 copy-start.53
  44.3 1.1 copy-start.54
  44.3 1.2 copy-start.66
  45.5 0.9 copy-start.36
  45.5 1.0 copy-start.37
  47.4 1.0 copy-start.16
  47.4 1.0 copy-start.47
  47.5 1.1 copy-start.48
  47.5 1.1 copy-start.63
  48.6 0.9 copy-start.30
  48.6 1.0 copy-start.31
  50.6 1.0 copy-start.43
  50.6 1.0 copy-start.44
  50.6 1.1 copy-start.61
  51.6 0.9 copy-start.26
  51.7 1.0 copy-start.27
  54.7 33.3 %all-to-all-start.1 = ((bf16[2,16,64,256]{3,2,0,1:T(8,128)(2,1)}), bf16[2,16,64,256]{3,2,0,1:T(8,128)(2,1)}, u32[]{:S(2)}, u32[]{:S(2)}) async-start(bf16[2,16,64,256]{3,2,0,1:T(8,128)(2,1)} %copy.55), calls=%async_computation.1 | async-start | bytes 2097152 | tf_op jit(solution)/shard_map/all_to_all | solution.py:145
  62.6 32.4 %copy-start.6 = (bf16[256,256]{1,0:T(8,128)(2,1)S(1)}, bf16[256,256]{1,0:T(8,128)(2,1)}, u32[]{:S(2)}) copy-start(bf16[256,256]{1,0:T(8,128)(2,1)} %get-tuple-element.151) | copy-start | bytes 393220
  62.6 32.4 %copy-start.23 = (bf16[256,256]{1,0:T(8,128)(2,1)S(1)}, bf16[256,256]{1,0:T(8,128)(2,1)}, u32[]{:S(2)}) copy-start(bf16[256,256]{1,0:T(8,128)(2,1)} %get-tuple-element.88) | copy-start | bytes 393220
  62.6 33.3 %copy-start.19 = (bf16[256,256]{1,0:T(8,128)(2,1)S(1)}, bf16[256,256]{1,0:T(8,128)(2,1)}, u32[]{:S(2)}) copy-start(bf16[256,256]{1,0:T(8,128)(2,1)} %get-tuple-element.165) | copy-start | bytes 393220
  88.0 22.4 %all-to-all-start.2 = ((bf16[2,16,64,256]{3,2,0,1:T(8,128)(2,1)}), bf16[2,16,64,256]{3,2,0,1:T(8,128)(2,1)S(1)}, u32[]{:S(2)}, u32[]{:S(2)}) async-start(bf16[2,16,64,256]{3,2,0,1:T(8,128)(2,1)} %all-to-all-done.1), calls=%async_computation.2 | async-start | bytes 2097152 | tf_op jit(solution)/shard_map/all_to_all | solution.py:148
  97.5 13.0 %copy-start.13 = (bf16[256,256]{1,0:T(8,128)(2,1)}, bf16[256,256]{1,0:T(8,128)(2,1)S(1)}, u32[]{:S(2)}) copy-start(bf16[256,256]{1,0:T(8,128)(2,1)S(1)} %get-tuple-element.167) | copy-start | bytes 393220
  97.5 13.0 %copy-start.17 = (bf16[256,256]{1,0:T(8,128)(2,1)}, bf16[256,256]{1,0:T(8,128)(2,1)S(1)}, u32[]{:S(2)}) copy-start(bf16[256,256]{1,0:T(8,128)(2,1)S(1)} %get-tuple-element.68) | copy-start | bytes 393220
  98.4 12.1 %copy-start.55 = (bf16[256,256]{1,0:T(8,128)(2,1)S(1)}, bf16[256,256]{1,0:T(8,128)(2,1)}, u32[]{:S(2)}) copy-start(bf16[256,256]{1,0:T(8,128)(2,1)} %get-tuple-element.149) | copy-start | bytes 393220
  98.4 12.1 %copy-start.57 = (bf16[256,256]{1,0:T(8,128)(2,1)S(1)}, bf16[256,256]{1,0:T(8,128)(2,1)}, u32[]{:S(2)}) copy-start(bf16[256,256]{1,0:T(8,128)(2,1)} %get-tuple-element.152) | copy-start | bytes 393220
  98.4 12.1 %copy-start.67 = (bf16[256,256]{1,0:T(8,128)(2,1)S(1)}, bf16[256,256]{1,0:T(8,128)(2,1)}, u32[]{:S(2)}) copy-start(bf16[256,256]{1,0:T(8,128)(2,1)} %get-tuple-element.87) | copy-start | bytes 393220
  110.5 1.0 copy-start.38
  110.6 1.0 copy-start.39
  110.6 1.0 copy-start.56
  110.6 1.1 copy-start.58
  110.6 1.1 copy-start.68
  112.6 1.0 copy-start.51
  112.6 1.0 copy-start.52
  112.6 1.1 copy-start.65
  113.7 0.9 copy-start.34
  113.7 1.0 copy-start.35
  115.7 1.0 copy-start.49
  115.7 1.0 copy-start.50
  115.7 1.1 copy-start.64
  116.8 0.9 copy-start.32
  116.8 1.0 copy-start.33
  118.7 1.0 copy-start.45
  118.7 1.0 copy-start.46
  118.7 1.1 copy-start.62
  119.8 1.0 copy-start.29
  121.9 19.4 %copy-start.42 = (bf16[2,16,1024]{2,1,0:T(8,128)(2,1)S(1)}, bf16[2,16,1024]{2,1,0:T(8,128)(2,1)}, u32[]{:S(2)}) copy-start(bf16[2,16,1024]{2,1,0:T(8,128)(2,1)} %param.6) | copy-start | bytes 196612
  (10 other events, 8.9 us)

commit v2 on v0

v2 whole, which is shorter than its diff:
```python
import functools

import jax
import jax.numpy as jnp
from jax import lax
from jax.experimental import pallas as pl
from jax.experimental.pallas import tpu as pltpu
from jax.sharding import PartitionSpec as P

MESH = pl.DeviceIdType.MESH
F32 = jnp.float32
BF16 = jnp.bfloat16
NZ, NY, NX, NC = 8, 4, 4, 2
NH = NY * NC
GROUP = NZ * NH
C = 256
CHUNKS = 2
KR = 16 // CHUNKS
AMP = 16
Z_ORDER = (4, 3, 5, 2, 6, 1, 7, 0)
Y_ORDER = (2, 1, 3, 0)


def position():
    sx = lax.axis_index("sx")
    sy = lax.axis_index("sy")
    return lax.rem(sx, 8), (sx // 8) * 2 + lax.rem(sy // 2, 2), sy // 4, lax.rem(sy, 2)


def device(z, y, x, c):
    return ((y // 2) * 8 + z, x * 4 + lax.rem(y, 2) * 2 + c)


def bits_index(y, c):
    return y // 2 + 2 * c + 4 * lax.rem(y, 2)


def ones(number):
    return bin(number).count("1")


def turned(block, power):
    power %= 4
    re, im = block[:, :C], block[:, C:]
    if power == 0:
        return block
    if power == 1:
        return jnp.concatenate([-im, re], axis=1)
    if power == 2:
        return -block
    return jnp.concatenate([im, -re], axis=1)


def hadamard(blocks):
    blocks = list(blocks)
    half = 1
    while half < len(blocks):
        for low in range(len(blocks)):
            if not low & half:
                a, b = blocks[low], blocks[low | half]
                blocks[low], blocks[low | half] = a + b, a - b
        half *= 2
    return blocks


def fill_full(full, index, re, im):
    full[index, :C, :C] = re
    full[index, :C, C:] = im
    full[index, C:, :C] = -im
    full[index, C:, C:] = re


def section_pairs(gates, first, right, tops):
    for which in range(2):
        tops[which, :, :C] = gates[first, which, 0]
        tops[which, :, C:] = gates[first, which, 1]
        fill_full(right, which, gates[first + 1, which, 0], gates[first + 1, which, 1])
    aa = jnp.dot(tops[0], right[0], preferred_element_type=F32)
    bb = jnp.dot(tops[1], right[1], preferred_element_type=F32)
    even, odd = aa - bb, aa + bb
    ba = jnp.dot(tops[1], right[0], preferred_element_type=F32)
    ab = jnp.dot(tops[0], right[1], preferred_element_type=F32)
    plus, minus = turned(ba + ab, -1), turned(ba - ab, -1)
    return even + plus, odd - minus, odd + minus, even - plus


def triple_products(gates, first, right, tops, full):
    for low, pair in enumerate(section_pairs(gates, first, right, tops)):
        tops[2 + low] = pair.astype(BF16)
    for which in range(2):
        fill_full(right, which, gates[first + 2, which, 0], gates[first + 2, which, 1])
    for low in range(4):
        with_a = jnp.dot(tops[2 + low], right[0], preferred_element_type=F32)
        with_b = turned(jnp.dot(tops[2 + low], right[1], preferred_element_type=F32), -1)
        for third, out in enumerate((with_a + with_b, with_a - with_b)):
            out = out.astype(BF16)
            fill_full(full, low + 4 * third, out[:, :C], out[:, C:])


def pair_products(gates, first, right, tops, full):
    for low, pair in enumerate(section_pairs(gates, first, right, tops)):
        pair = pair.astype(BF16)
        fill_full(full, low, pair[:, :C], pair[:, C:])


def wait_bytes(ref, sem):
    pltpu.make_async_copy(ref, ref, sem).wait()


def sections(q, recv, work1, work2, g_low, g_high, ret_send):
    def forward_z(h, carry):
        blocks = []
        for z in range(NZ):
            both = recv[q, h * NZ + z].astype(F32)
            blocks.append(turned(jnp.concatenate([both[0], both[1]], axis=1), ones(z)))
        for t, block in enumerate(hadamard(blocks)):
            work1[h, t] = block
        return carry

    def forward_h(t, carry):
        blocks = hadamard([turned(work1[h, t], ones(h)) for h in range(NH)])
        left = jnp.concatenate(blocks, axis=0).astype(BF16)
        out = jnp.dot(left, g_low[t], preferred_element_type=F32)
        for h in range(NH):
            work2[h, t] = out[h * KR : (h + 1) * KR]
        return carry

    def inverse_z(h, carry):
        left = work2[h].reshape(NZ * KR, 2 * C).astype(BF16)
        out = jnp.dot(left, g_high[h], preferred_element_type=F32)
        blocks = hadamard([out[t * KR : (t + 1) * KR] for t in range(NZ)])
        for z in range(NZ):
            work1[h, z] = turned(blocks[z], -ones(z))
        return carry

    def inverse_h(z, carry):
        blocks = hadamard([work1[t, z] for t in range(NH)])
        for h in range(NH):
            ret_send[q, h, z] = (turned(blocks[h], -ones(h)) * (1.0 / GROUP)).astype(BF16)
        return carry

    lax.fori_loop(0, NH, forward_z, 0)
    lax.fori_loop(0, NZ, forward_h, 0)
    lax.fori_loop(0, NH, inverse_z, 0)
    lax.fori_loop(0, NZ, inverse_h, 0)


def kernel(
    x_ref, gates_ref, rows_ref, cols_ref, out_ref,
    recv, work1, work2, ret_send, ret, gates, right, tops, g_low, g_high, g_x,
    cols, crx, ccx, wbuf, finz, finx,
    local_sem, main_send, main_recv, small_send, small_recv, x_send, x_recv, back_send, back_recv, fin_send, fin_recv,
):
    mz, my, mx, mc = position()
    mh = bits_index(my, mc)
    mine = mh * NZ + mz

    z_peers = [lax.rem(mz + d, NZ) for d in range(NZ)]
    y_peers = [lax.rem(my + d, NY) for d in range(NY)]
    c_peers = [lax.rem(mc + d, NC) for d in range(NC)]
    x_peers = [lax.rem(mx + d, NX) for d in range(NX)]
    group = [(dz, dy, dc) for dz in Z_ORDER for dy in Y_ORDER for dc in range(NC) if dz or dy or dc]
    back = [(dy, dc) for dy in Y_ORDER for dc in range(NC) if dy or dc]

    barrier = pltpu.get_barrier_semaphore()
    for dz, dy, dc in group:
        pl.semaphore_signal(barrier, inc=1, device_id=device(z_peers[dz], y_peers[dy], mx, c_peers[dc]), device_id_type=MESH)
    for dx in range(1, NX):
        pl.semaphore_signal(barrier, inc=1, device_id=device(mz, my, x_peers[dx], mc), device_id_type=MESH)

    gates_copy = pltpu.make_async_copy(gates_ref, gates, local_sem.at[0])
    gates_copy.start()
    cols_copy = pltpu.make_async_copy(cols_ref, cols, local_sem.at[1])
    cols_copy.start()
    own_rows = pltpu.make_async_copy(rows_ref.at[:, :, pl.ds(pl.multiple_of(mz * 128, 128), 128)], crx.at[mx, mz], local_sem.at[2])
    own_rows.start()
    own = []
    for q in range(CHUNKS):
        copy = pltpu.make_async_copy(x_ref.at[:, mz * NH + mh, q], recv.at[q, mine], local_sem.at[3 + q])
        copy.start()
        own.append(copy)
    cols_copy.wait()
    ccx[mx, mz] = cols[...].astype(BF16)
    gates_copy.wait()
    triple_products(gates, 0, right, tops, g_low)
    pl.semaphore_wait(barrier, GROUP - 1 + NX - 1)

    def remote(src, dst, send, recv_sem, where):
        copy = pltpu.make_async_remote_copy(
            src_ref=src, dst_ref=dst, send_sem=send, recv_sem=recv_sem, device_id=device(*where), device_id_type=MESH
        )
        copy.start()

    for dz in Z_ORDER[:-1]:
        pz = z_peers[dz]
        there = (pz, my, mx, mc)
        columns = pl.ds(pl.multiple_of(pz * 128, 128), 128)
        remote(rows_ref.at[:, :, columns], crx.at[mx, mz], small_send.at[0], small_recv.at[0], there)
        remote(ccx.at[mx, mz], ccx.at[mx, mz], small_send.at[1], small_recv.at[1], there)
    for q in range(CHUNKS):
        for dz, dy, dc in group:
            pz, py, pc = z_peers[dz], y_peers[dy], c_peers[dc]
            block = pz * NH + bits_index(py, pc)
            remote(x_ref.at[:, block, q], recv.at[q, mine], main_send.at[q], main_recv.at[q], (pz, py, mx, pc))

    triple_products(gates, 3, right, tops, g_high)
    pair_products(gates, 6, right, tops, g_x)

    own_rows.wait()
    wait_bytes(crx.at[0, pl.ds(0, NZ - 1)], small_recv.at[0])
    wait_bytes(ccx.at[0, pl.ds(0, NZ - 1)], small_recv.at[1])
    for dx in (2, 1, 3):
        there = (mz, my, x_peers[dx], mc)
        remote(crx.at[mx], crx.at[mx], x_send.at[0], x_recv.at[0], there)
        remote(ccx.at[mx], ccx.at[mx], x_send.at[1], x_recv.at[1], there)

    def columns_through_x():
        m0, m1 = lax.rem(mx, 2), mx // 2
        for xs in range(NX):
            parts = []
            for z in range(NZ):
                both = ccx[xs, z]
                parts.append(jnp.concatenate([both[0], -both[1]], axis=1))
            left = jnp.concatenate(parts, axis=0)
            s0, s1 = xs % 2, xs // 2
            e0 = s0 + m0 - 2 * s0 * m0
            e1 = s1 + m1 - 2 * s1 * m1
            f0 = (1 - 2 * e0).astype(F32)
            f1 = (1 - 2 * e1).astype(F32)
            turn = lax.rem(m0 + m1 - s0 - s1 + 4, 4)
            odd = lax.rem(turn, 2)
            cos = ((1 - odd) * (1 - turn)).astype(F32)
            sin = (odd * (2 - turn)).astype(F32)
            total = None
            for t in range(4):
                u = lax.dot_general(left, g_x[t], (((1,), (1,)), ((), ())), preferred_element_type=F32)
                if t & 1:
                    u = u * f0
                if t & 2:
                    u = u * f1
                total = u if total is None else total + u
            total = total * 0.25
            re, neg_im = total[:, :C], total[:, C:]
            new_re = cos * re + sin * neg_im
            new_neg = cos * neg_im - sin * re
            for z in range(NZ):
                wbuf[z, xs * AMP : (xs + 1) * AMP, :C] = new_re[z * AMP : (z + 1) * AMP]
                wbuf[z, xs * AMP : (xs + 1) * AMP, C:] = new_neg[z * AMP : (z + 1) * AMP]

    for q in range(CHUNKS):
        own[q].wait()
        wait_bytes(recv.at[q, pl.ds(0, GROUP - 1)], main_recv.at[q])
        sections(q, recv, work1, work2, g_low, g_high, ret_send)
        for dy, dc in back:
            py, pc = y_peers[dy], c_peers[dc]
            remote(ret_send.at[q, bits_index(py, pc)], ret.at[q, mh], back_send.at[q], back_recv.at[q], (mz, py, mx, pc))
        ret[q, mh] = ret_send[q, mh]
        if q == 0:
            wait_bytes(crx.at[pl.ds(0, NX - 1)], x_recv.at[0])
            wait_bytes(ccx.at[pl.ds(0, NX - 1)], x_recv.at[1])
            columns_through_x()

    for q in range(CHUNKS):
        wait_bytes(ret.at[q, pl.ds(0, NH - 1)], back_recv.at[q])

    def close(z, carry):
        blocks = []
        for h in range(NH):
            for q in range(CHUNKS):
                blocks.append(ret[q, h, z].astype(F32))
        tensor = jnp.concatenate(blocks, axis=0).astype(BF16)
        rows = []
        for part in range(2):
            for xs in range(NX):
                rows.append(crx[xs, z, part])
        proj = jnp.dot(jnp.concatenate(rows, axis=0), tensor, preferred_element_type=F32)
        half = NX * AMP
        p_re = proj[:half, :C] - proj[half:, C:]
        p_im = proj[:half, C:] + proj[half:, :C]
        w = wbuf[z]
        w_re, w_neg = w[:, :C], w[:, C:]
        a_re = p_re * w_re + p_im * w_neg
        a_im = p_im * w_re - p_re * w_neg
        both = jnp.concatenate([a_re[:, :128] + a_re[:, 128:], a_im[:, :128] + a_im[:, 128:]], axis=0)
        finz[mz, pl.ds(z, 1)] = jnp.sum(jnp.transpose(both), axis=0, keepdims=True)
        return carry

    lax.fori_loop(0, NZ, close, 0)

    wait_bytes(crx.at[0, pl.ds(0, NZ - 1)], small_send.at[0])
    wait_bytes(ccx.at[0, pl.ds(0, NZ - 1)], small_send.at[1])
    wait_bytes(crx.at[pl.ds(0, NX - 1)], x_send.at[0])
    wait_bytes(ccx.at[pl.ds(0, NX - 1)], x_send.at[1])
    for q in range(CHUNKS):
        wait_bytes(recv.at[q, pl.ds(0, GROUP - 1)], main_send.at[q])
        wait_bytes(ret.at[q, pl.ds(0, NH - 1)], back_send.at[q])

    for dz in Z_ORDER[:-1]:
        remote(finz.at[mz], finz.at[mz], fin_send.at[0], fin_recv.at[0], (z_peers[dz], my, mx, mc))
    wait_bytes(finz.at[pl.ds(0, NZ - 1)], fin_recv.at[0])
    finx[mx] = jnp.sum(finz[...], axis=0)
    wait_bytes(finz.at[pl.ds(0, NZ - 1)], fin_send.at[0])
    for dx in (2, 1, 3):
        remote(finx.at[mx], finx.at[mx], fin_send.at[1], fin_recv.at[1], (mz, my, x_peers[dx], mc))
    wait_bytes(finx.at[pl.ds(0, NX - 1)], fin_recv.at[1])
    out_ref[mh] = jnp.sum(finx[...], axis=0)
    wait_bytes(finx.at[pl.ds(0, NX - 1)], fin_send.at[1])
    for dy, dc in back:
        remote(out_ref.at[mh], out_ref.at[mh], fin_send.at[2], fin_recv.at[2], (mz, y_peers[dy], mx, c_peers[dc]))
    wait_bytes(out_ref.at[pl.ds(0, NH - 1)], fin_recv.at[2])
    wait_bytes(out_ref.at[pl.ds(0, NH - 1)], fin_send.at[2])


def local(tensors, gates, closing_rows, closing_columns):
    dma = pltpu.SemaphoreType.DMA
    out = pl.pallas_call(
        kernel,
        out_shape=jax.ShapeDtypeStruct((NH, NZ, 128), F32),
        in_specs=[pl.BlockSpec(memory_space=pl.ANY)] * 4,
        out_specs=pl.BlockSpec(memory_space=pltpu.VMEM),
        scratch_shapes=[
            pltpu.VMEM((CHUNKS, GROUP, 2, KR, C), BF16),
            pltpu.VMEM((NH, NZ, KR, 2 * C), F32),
            pltpu.VMEM((NH, NZ, KR, 2 * C), F32),
            pltpu.VMEM((CHUNKS, NH, NZ, KR, 2 * C), BF16),
            pltpu.VMEM((CHUNKS, NH, NZ, KR, 2 * C), BF16),
            pltpu.VMEM((8, 2, 2, C, C), BF16),
            pltpu.VMEM((2, 2 * C, 2 * C), BF16),
            pltpu.VMEM((6, C, 2 * C), BF16),
            pltpu.VMEM((8, 2 * C, 2 * C), BF16),
            pltpu.VMEM((8, 2 * C, 2 * C), BF16),
            pltpu.VMEM((4, 2 * C, 2 * C), BF16),
            pltpu.VMEM((2, AMP, C), F32),
            pltpu.VMEM((NX, NZ, 2, AMP, 128), BF16),
            pltpu.VMEM((NX, NZ, 2, AMP, C), BF16),
            pltpu.VMEM((NZ, NX * AMP, 2 * C), F32),
            pltpu.VMEM((NZ, NZ, 128), F32),
            pltpu.VMEM((NX, NZ, 128), F32),
            dma((3 + CHUNKS,)),
            dma((CHUNKS,)),
            dma((CHUNKS,)),
            dma((2,)),
            dma((2,)),
            dma((2,)),
            dma((2,)),
            dma((CHUNKS,)),
            dma((CHUNKS,)),
            dma((3,)),
            dma((3,)),
        ],
        compiler_params=pltpu.CompilerParams(
            collective_id=0, has_side_effects=True, vmem_limit_bytes=56 * 1024 * 1024
        ),
        name="network",
    )(
        tensors.reshape(2, GROUP, CHUNKS, KR, C),
        gates,
        closing_rows,
        closing_columns,
    )
    out = out.reshape(2, 2, 2, NZ, 2, NX, AMP).transpose(4, 2, 3, 5, 0, 1, 6)
    return out.reshape(2, -1)


def solution(mesh):
    placed = (
        P(None, "sx", "sy", None, None),
        P(),
        P(None, ("sx", "sy"), None),
        P(None, ("sx", "sy"), None),
    )
    return jax.shard_map(local, mesh=mesh, in_specs=placed, out_specs=P(), check_vma=False)
```

time: 486 us -> 70.3 us (0.14)
  blocking collectives: 361 us -> 0 us
  Pallas kernels: 0 us -> 68.1 us
  waiting for transfers between devices: 54.8 us -> 0 us
  starting transfers between devices: 24.8 us -> 0 us
  local copies, waits for them, and re-layouts: 21.2 us -> 2.12 us
  matrix products: 12.2 us -> 0 us
  other arithmetic: 10.1 us -> 0 us
    all_gather x1 -> x0, blocking collectives: 342 us -> none  [local(): return lax.all_gather(closed, ('sx', 'sy'), axis=1, tiled=True)]
    pallas_call x0 -> x1, Pallas kernels: none -> 68.1 us  [local(): pl.pallas_call(kernel, out_shape=jax.ShapeDtypeStruct((NH, NZ, 128), F32)...]
    all_to_all x3 -> x0, waiting for transfers between devices: 54.8 us -> none  [the longest x1 25.4 us: local(): lax.all_to_all(grouped, 'sx', split_axis=1, concat_axis=1, tiled=True)]
    all_to_all x3 -> x0, starting transfers between devices: 24.8 us -> none  [the longest x1 11.7 us: local(): lax.all_to_all(current.reshape(2, count_x, rows_dev // count_x, width), '...]
    all_to_all x1 -> x0, blocking collectives: 19.4 us -> none  [local(): lax.all_to_all(grouped, 'sy', split_axis=1, concat_axis=1, tiled=True)]
    dot_general x20 -> x0, matrix products: 12.2 us -> none  [the longest x16 11.3 us: combine(): jnp.dot(joined, matrix, preferred_element_type=jnp.float32)]
    unnamed x137 -> x0, local copies, waits for them, and re-layouts: 10.4 us -> none
    squeeze x5 -> x0, local copies, waits for them, and re-layouts: 6.04 us -> none  [the longest x4 3.56 us: mixing_matrix(): own_top = jnp.concatenate([gate_pair[0, 0], gate_pair[0, 1]], axis=1)]
  transfers between devices with their start and end apart: 3 -> 0, of which waited for: 3 -> 0; matrix products, arithmetic and copies ran while one was open for 3% -> 0% of each run, Pallas kernels for 0% -> 0%
where the time goes in v2:
time: 70.3 us; the launch traced here: 70.2 us
  Pallas kernels  68.1 us (97%)
  local copies, waits for them, and re-layouts  2.12 us (3%)
    pallas_call x1, Pallas kernels, local(): pl.pallas_call(kernel, out_shape=jax.ShapeDtypeStruct((NH, NZ, 128), F32)...  68.1 us

profile of v2, /device:TPU:1, one launch (start us, length us, event | category | flops | bytes accessed | tf_op | source)
XLA Modules:
  0.0 70.2 jit_solution(8086747582024524584)
XLA Ops:
  0.0 68.1 %network.1 = f32[8,8,128]{2,1,0:T(8,128)} custom-call(bf16[2,64,2,8,256]{4,3,2,1,0:T(8,128)(2,1)} %bitcast.3, bf16[8,2,2,256,256]{4,3,2,1,0:T(8,128)(2,1)} %gates_ref.1, bf16[2,16,1024]{2,1,0:T(8,128)(2,1)} %rows_ref.1, f32[2,16,256]{2,1,0:T(8,128)} %cols_ref.1), custom_call_target="tpu_custom_call" | custom-call | tf_op jit(solution)/shard_map/network/pallas_call | solution.py:316
  68.1 1.0 %reshape.10 = f32[2,2,2,8,2,4,16]{6,5,4,3,2,1,0:T(4,128)S(1)} reshape(f32[8,8,128]{2,1,0:T(8,128)} %network.1) | data formatting | bytes 65536 | tf_op jit(solution)/shard_map/reshape | solution.py:361
  69.0 0.2 copy.5
  69.2 0.9 %reshape.11 = f32[2,4096]{1,0:T(2,128)} reshape(f32[2,2,8,4,2,2,16]{6,5,4,3,2,1,0:T(2,128)S(1)} %copy.5) | data formatting | bytes 65536 | tf_op jit(solution)/shard_map/reshape | solution.py:362

commit v3 on v2

v3 whole, which is shorter than its diff:
```python
import functools

import jax
import jax.numpy as jnp
from jax import lax
from jax.experimental import pallas as pl
from jax.experimental.pallas import tpu as pltpu
from jax.sharding import PartitionSpec as P

MESH = pl.DeviceIdType.MESH
F32 = jnp.float32
BF16 = jnp.bfloat16
NZ, NY, NX, NC = 8, 4, 4, 2
NH = NY * NC
GROUP = NZ * NH
C = 256
CHUNKS = 4
KR = 4
UNROLL = True
AMP = 16
Z_ORDER = (4, 3, 5, 2, 6, 1, 7, 0)
Y_ORDER = (2, 1, 3, 0)


def position():
    sx = lax.axis_index("sx")
    sy = lax.axis_index("sy")
    return lax.rem(sx, 8), (sx // 8) * 2 + lax.rem(sy // 2, 2), sy // 4, lax.rem(sy, 2)


def device(z, y, x, c):
    return ((y // 2) * 8 + z, x * 4 + lax.rem(y, 2) * 2 + c)


def bits_index(y, c):
    return y // 2 + 2 * c + 4 * lax.rem(y, 2)


def ones(number):
    return bin(number).count("1")


def turned(block, power):
    power %= 4
    re, im = block[:, :C], block[:, C:]
    if power == 0:
        return block
    if power == 1:
        return jnp.concatenate([-im, re], axis=1)
    if power == 2:
        return -block
    return jnp.concatenate([im, -re], axis=1)


def hadamard(blocks):
    blocks = list(blocks)
    half = 1
    while half < len(blocks):
        for low in range(len(blocks)):
            if not low & half:
                a, b = blocks[low], blocks[low | half]
                blocks[low], blocks[low | half] = a + b, a - b
        half *= 2
    return blocks


def fill_full(full, index, re, im):
    full[index, :C, :C] = re
    full[index, :C, C:] = im
    full[index, C:, :C] = -im
    full[index, C:, C:] = re


def section_pairs(gates, first, right, tops):
    for which in range(2):
        tops[which, :, :C] = gates[first, which, 0]
        tops[which, :, C:] = gates[first, which, 1]
        fill_full(right, which, gates[first + 1, which, 0], gates[first + 1, which, 1])
    aa = jnp.dot(tops[0], right[0], preferred_element_type=F32)
    bb = jnp.dot(tops[1], right[1], preferred_element_type=F32)
    even, odd = aa - bb, aa + bb
    ba = jnp.dot(tops[1], right[0], preferred_element_type=F32)
    ab = jnp.dot(tops[0], right[1], preferred_element_type=F32)
    plus, minus = turned(ba + ab, -1), turned(ba - ab, -1)
    return even + plus, odd - minus, odd + minus, even - plus


def triple_products(gates, first, right, tops, full):
    for low, pair in enumerate(section_pairs(gates, first, right, tops)):
        tops[2 + low] = pair.astype(BF16)
    for which in range(2):
        fill_full(right, which, gates[first + 2, which, 0], gates[first + 2, which, 1])
    for low in range(4):
        with_a = jnp.dot(tops[2 + low], right[0], preferred_element_type=F32)
        with_b = turned(jnp.dot(tops[2 + low], right[1], preferred_element_type=F32), -1)
        for third, out in enumerate((with_a + with_b, with_a - with_b)):
            out = out.astype(BF16)
            full[low + 4 * third] = out


def pair_products(gates, first, right, tops, full):
    for low, pair in enumerate(section_pairs(gates, first, right, tops)):
        pair = pair.astype(BF16)
        fill_full(full, low, pair[:, :C], pair[:, C:])


def wait_bytes(ref, sem):
    pltpu.make_async_copy(ref, ref, sem).wait()


def half_turn(block):
    return pltpu.roll(block, KR, 0)


def times_gate(blocks, gate):
    left = jnp.concatenate(blocks, axis=0).astype(BF16)
    out = jnp.dot(left, gate, preferred_element_type=F32)
    sign = jnp.where(lax.broadcasted_iota(jnp.int32, (2 * KR, C), 0) < KR, -1.0, 1.0)
    result = []
    for n in range(len(blocks)):
        rows = out[n * 2 * KR : (n + 1) * 2 * KR]
        result.append(rows[:, :C] + sign * half_turn(rows[:, C:]))
    return result


def sections(q, recv, work1, work2, g_low, g_high, ret_send):
    def forward_z(h, carry):
        blocks = hadamard([recv[q, h * NZ + z].astype(F32) for z in range(NZ)])
        for t in range(NZ):
            work1[h, t] = blocks[t]
        return carry

    def forward_h(t, carry):
        blocks = times_gate(hadamard([work1[h, t] for h in range(NH)]), g_low[t])
        for h in range(NH):
            work2[h, t] = blocks[h]
        return carry

    def inverse_z(h, carry):
        blocks = hadamard(times_gate([work2[h, t] for t in range(NZ)], g_high[h]))
        for z in range(NZ):
            work1[h, z] = blocks[z]
        return carry

    def inverse_h(z, carry):
        blocks = hadamard([work1[t, z] for t in range(NH)])
        for h in range(NH):
            ret_send[q, h, z] = (blocks[h] * (1.0 / GROUP)).astype(BF16)
        return carry

    lax.fori_loop(0, NH, forward_z, 0, unroll=UNROLL)
    lax.fori_loop(0, NZ, forward_h, 0, unroll=UNROLL)
    lax.fori_loop(0, NH, inverse_z, 0, unroll=UNROLL)
    lax.fori_loop(0, NZ, inverse_h, 0, unroll=UNROLL)


def unit(turn):
    turn = lax.rem(turn, 4)
    odd = lax.rem(turn, 2)
    return ((1 - odd) * (1 - turn)).astype(F32), (odd * (2 - turn)).astype(F32)


def assemble(gathered, out_ref):
    lane = lax.broadcasted_iota(jnp.int32, (NZ, 128), 1) // AMP
    for part in range(2):
        for y_hi in range(2):
            for x_hi in range(2):
                total = None
                for x_lo in range(2):
                    for y_lo in range(2):
                        for core in range(2):
                            source = part * 4 + x_hi * 2 + x_lo
                            target = x_lo * 4 + y_lo * 2 + core
                            rows = gathered[y_hi + 2 * core + 4 * y_lo]
                            shift = (target - source) * AMP % 128
                            moved = pltpu.roll(rows, shift, 1) if shift else rows
                            total = moved if total is None else jnp.where(lane == target, moved, total)
                for z in range(NZ):
                    group = (y_hi * NZ + z) * 2 + x_hi
                    out_ref[part : part + 1, group * 128 : (group + 1) * 128] = total[z : z + 1]


def kernel(
    x_ref, gates_ref, rows_ref, cols_ref, out_ref,
    x_in, staged, recv, work1, work2, ret_send, ret, gates, right, tops, g_low, g_high, g_x,
    cols, crx, ccx, left, wbuf, finz, finx, finh,
    local_sem, main_send, main_recv, small_send, small_recv, x_send, x_recv, back_send, back_recv, fin_send, fin_recv,
):
    mz, my, mx, mc = position()
    mh = bits_index(my, mc)
    mine = mh * NZ + mz
    z0, z1, z2 = lax.rem(mz, 2), lax.rem(mz // 2, 2), mz // 4
    h_ones = my // 2 + lax.rem(my, 2) + mc

    z_peers = [lax.rem(mz + d, NZ) for d in range(NZ)]
    y_peers = [lax.rem(my + d, NY) for d in range(NY)]
    c_peers = [lax.rem(mc + d, NC) for d in range(NC)]
    x_peers = [lax.rem(mx + d, NX) for d in range(NX)]
    group = [(dz, dy, dc) for dz in Z_ORDER for dy in Y_ORDER for dc in range(NC) if dz or dy or dc]
    back = [(dy, dc) for dy in Y_ORDER for dc in range(NC) if dy or dc]

    x_copy = pltpu.make_async_copy(x_ref, x_in, local_sem.at[3])
    x_copy.start()
    cols_copy = pltpu.make_async_copy(cols_ref, cols, local_sem.at[1])
    cols_copy.start()
    own_rows = pltpu.make_async_copy(rows_ref.at[:, :, pl.ds(pl.multiple_of(mz * 128, 128), 128)], crx.at[mx, mz], local_sem.at[2])
    own_rows.start()
    gates_copy = pltpu.make_async_copy(gates_ref, gates, local_sem.at[0])
    gates_copy.start()

    barrier = pltpu.get_barrier_semaphore()
    for dz, dy, dc in group:
        pl.semaphore_signal(barrier, inc=1, device_id=device(z_peers[dz], y_peers[dy], mx, c_peers[dc]), device_id_type=MESH)
    for dx in range(1, NX):
        pl.semaphore_signal(barrier, inc=1, device_id=device(mz, my, x_peers[dx], mc), device_id_type=MESH)

    cos, sin = unit(z0 + z1 + z2 + h_ones)
    low = lax.broadcasted_iota(jnp.int32, (2 * KR, C), 0) < KR

    def stage(target, carry):
        re = x_in[0, target].astype(F32)
        im = x_in[1, target].astype(F32)
        re, im = cos * re - sin * im, cos * im + sin * re
        for half in range(2):
            a, b = re[8 * half : 8 * half + 8], im[8 * half : 8 * half + 8]
            staged[2 * half, target] = jnp.where(low, a, half_turn(b)).astype(BF16)
            staged[2 * half + 1, target] = jnp.where(low, half_turn(a), b).astype(BF16)
        return carry

    cols_copy.wait()
    ccx[mx, mz] = cols[...].astype(BF16)
    x_copy.wait()
    lax.fori_loop(0, GROUP, stage, 0, unroll=4)
    for q in range(CHUNKS):
        recv[q, mine] = staged[q, mz * NH + mh]
    pl.semaphore_wait(barrier, GROUP - 1 + NX - 1)

    def remote(src, dst, send, recv_sem, where):
        copy = pltpu.make_async_remote_copy(
            src_ref=src, dst_ref=dst, send_sem=send, recv_sem=recv_sem, device_id=device(*where), device_id_type=MESH
        )
        copy.start()

    for dz in Z_ORDER[:-1]:
        pz = z_peers[dz]
        there = (pz, my, mx, mc)
        columns = pl.ds(pl.multiple_of(pz * 128, 128), 128)
        remote(rows_ref.at[:, :, columns], crx.at[mx, mz], small_send.at[0], small_recv.at[0], there)
        remote(ccx.at[mx, mz], ccx.at[mx, mz], small_send.at[1], small_recv.at[1], there)
    for q in range(CHUNKS):
        for dz, dy, dc in group:
            pz, py, pc = z_peers[dz], y_peers[dy], c_peers[dc]
            block = pz * NH + bits_index(py, pc)
            remote(staged.at[q, block], recv.at[q, mine], main_send.at[q], main_recv.at[q], (pz, py, mx, pc))

    gates_copy.wait()
    triple_products(gates, 0, right, tops, g_low)
    triple_products(gates, 3, right, tops, g_high)
    pair_products(gates, 6, right, tops, g_x)

    own_rows.wait()
    wait_bytes(crx.at[0, pl.ds(0, NZ - 1)], small_recv.at[0])
    wait_bytes(ccx.at[0, pl.ds(0, NZ - 1)], small_recv.at[1])
    for dx in (2, 1, 3):
        there = (mz, my, x_peers[dx], mc)
        remote(crx.at[mx], crx.at[mx], x_send.at[0], x_recv.at[0], there)
        remote(ccx.at[mx], ccx.at[mx], x_send.at[1], x_recv.at[1], there)

    def closing_rows_in_order():
        row = lax.broadcasted_iota(jnp.int32, (128, 2 * C), 0)
        column = lax.broadcasted_iota(jnp.int32, (128, 2 * C), 1)
        wanted = (row // KR) * 2 * KR + lax.rem(row, KR)
        wanted = jnp.where(column < C, wanted, wanted + C + KR)
        select = jnp.where(column == wanted, 1.0, 0.0).astype(BF16)
        for z in range(NZ):
            rows = [crx[xs, z, part] for part in range(2) for xs in range(NX)]
            out = jnp.dot(jnp.concatenate(rows, axis=0), select, preferred_element_type=F32)
            half = NX * AMP
            for_re = out[:half, :C] - out[half:, C:]
            for_im = out[half:, :C] + out[:half, C:]
            left[z] = jnp.concatenate([for_re, for_im], axis=0).astype(BF16)

    def columns_through_x():
        m0, m1 = lax.rem(mx, 2), mx // 2
        for xs in range(NX):
            parts = []
            for z in range(NZ):
                both = ccx[xs, z]
                parts.append(jnp.concatenate([both[0], -both[1]], axis=1))
            vectors = jnp.concatenate(parts, axis=0)
            s0, s1 = xs % 2, xs // 2
            e0 = s0 + m0 - 2 * s0 * m0
            e1 = s1 + m1 - 2 * s1 * m1
            f0 = (1 - 2 * e0).astype(F32)
            f1 = (1 - 2 * e1).astype(F32)
            cos, sin = unit(m0 + m1 - s0 - s1 - h_ones + 8)
            total = None
            for t in range(4):
                u = lax.dot_general(vectors, g_x[t], (((1,), (1,)), ((), ())), preferred_element_type=F32)
                if t & 1:
                    u = u * f0
                if t & 2:
                    u = u * f1
                total = u if total is None else total + u
            total = total * 0.25
            re, neg = total[:, :C], total[:, C:]
            re, neg = cos * re + sin * neg, cos * neg - sin * re
            for z in range(NZ):
                a, b = re[z * AMP : (z + 1) * AMP], neg[z * AMP : (z + 1) * AMP]
                a, b = ((a, b), (-b, a), (-a, -b), (b, -a))[ones(z)]
                wbuf[z, xs * AMP : (xs + 1) * AMP, :C] = a
                wbuf[z, xs * AMP : (xs + 1) * AMP, C:] = b

    for q in range(CHUNKS):
        wait_bytes(recv.at[q, pl.ds(0, GROUP - 1)], main_recv.at[q])
        sections(q, recv, work1, work2, g_low, g_high, ret_send)
        for dy, dc in back:
            py, pc = y_peers[dy], c_peers[dc]
            remote(ret_send.at[q, bits_index(py, pc)], ret.at[q, mh], back_send.at[q], back_recv.at[q], (mz, py, mx, pc))
        ret[q, mh] = ret_send[q, mh]
        if q == 0:
            wait_bytes(crx.at[pl.ds(0, NX - 1)], x_recv.at[0])
            wait_bytes(ccx.at[pl.ds(0, NX - 1)], x_recv.at[1])
            closing_rows_in_order()
            columns_through_x()

    for q in range(CHUNKS):
        wait_bytes(ret.at[q, pl.ds(0, NH - 1)], back_recv.at[q])

    def close(z, carry):
        blocks = []
        for h in range(NH):
            for q in range(CHUNKS):
                blocks.append(ret[q, h, z].astype(F32))
        tensor = jnp.concatenate(blocks, axis=0).astype(BF16)
        proj = jnp.dot(left[z], tensor, preferred_element_type=F32)
        half = NX * AMP
        p_re, p_im = proj[:half], proj[half:]
        w = wbuf[z]
        w_re, w_neg = w[:, :C], w[:, C:]
        a_re = p_re * w_re + p_im * w_neg
        a_im = p_im * w_re - p_re * w_neg
        both = jnp.concatenate([a_re[:, :128] + a_re[:, 128:], a_im[:, :128] + a_im[:, 128:]], axis=0)
        finz[mz, pl.ds(z, 1)] = jnp.sum(jnp.transpose(both), axis=0, keepdims=True)
        return carry

    lax.fori_loop(0, NZ, close, 0, unroll=UNROLL)

    for dz in Z_ORDER[:-1]:
        remote(finz.at[mz], finz.at[mz], fin_send.at[0], fin_recv.at[0], (z_peers[dz], my, mx, mc))
    wait_bytes(crx.at[0, pl.ds(0, NZ - 1)], small_send.at[0])
    wait_bytes(ccx.at[0, pl.ds(0, NZ - 1)], small_send.at[1])
    wait_bytes(crx.at[pl.ds(0, NX - 1)], x_send.at[0])
    wait_bytes(ccx.at[pl.ds(0, NX - 1)], x_send.at[1])
    for q in range(CHUNKS):
        wait_bytes(recv.at[q, pl.ds(0, GROUP - 1)], main_send.at[q])
        wait_bytes(ret.at[q, pl.ds(0, NH - 1)], back_send.at[q])
    wait_bytes(finz.at[pl.ds(0, NZ - 1)], fin_recv.at[0])
    finx[mx] = jnp.sum(finz[...], axis=0)
    for dx in (2, 1, 3):
        remote(finx.at[mx], finx.at[mx], fin_send.at[1], fin_recv.at[1], (mz, my, x_peers[dx], mc))
    wait_bytes(finz.at[pl.ds(0, NZ - 1)], fin_send.at[0])
    wait_bytes(finx.at[pl.ds(0, NX - 1)], fin_recv.at[1])
    finh[mh] = jnp.sum(finx[...], axis=0)
    for dy, dc in back:
        remote(finh.at[mh], finh.at[mh], fin_send.at[2], fin_recv.at[2], (mz, y_peers[dy], mx, c_peers[dc]))
    wait_bytes(finx.at[pl.ds(0, NX - 1)], fin_send.at[1])
    wait_bytes(finh.at[pl.ds(0, NH - 1)], fin_recv.at[2])
    assemble(finh, out_ref)
    wait_bytes(finh.at[pl.ds(0, NH - 1)], fin_send.at[2])


def local(tensors, gates, closing_rows, closing_columns):
    dma = pltpu.SemaphoreType.DMA
    return pl.pallas_call(
        kernel,
        out_shape=jax.ShapeDtypeStruct((2, NZ * NH * NX * AMP), F32),
        in_specs=[pl.BlockSpec(memory_space=pl.ANY)] * 4,
        out_specs=pl.BlockSpec(memory_space=pltpu.VMEM),
        scratch_shapes=[
            pltpu.VMEM((2, GROUP, 16, C), BF16),
            pltpu.VMEM((CHUNKS, GROUP, 2 * KR, C), BF16),
            pltpu.VMEM((CHUNKS, GROUP, 2 * KR, C), BF16),
            pltpu.VMEM((NH, NZ, 2 * KR, C), F32),
            pltpu.VMEM((NH, NZ, 2 * KR, C), F32),
            pltpu.VMEM((CHUNKS, NH, NZ, 2 * KR, C), BF16),
            pltpu.VMEM((CHUNKS, NH, NZ, 2 * KR, C), BF16),
            pltpu.VMEM((8, 2, 2, C, C), BF16),
            pltpu.VMEM((2, 2 * C, 2 * C), BF16),
            pltpu.VMEM((6, C, 2 * C), BF16),
            pltpu.VMEM((8, C, 2 * C), BF16),
            pltpu.VMEM((8, C, 2 * C), BF16),
            pltpu.VMEM((4, 2 * C, 2 * C), BF16),
            pltpu.VMEM((2, AMP, C), F32),
            pltpu.VMEM((NX, NZ, 2, AMP, 128), BF16),
            pltpu.VMEM((NX, NZ, 2, AMP, C), BF16),
            pltpu.VMEM((NZ, 128, C), BF16),
            pltpu.VMEM((NZ, NX * AMP, 2 * C), F32),
            pltpu.VMEM((NZ, NZ, 128), F32),
            pltpu.VMEM((NX, NZ, 128), F32),
            pltpu.VMEM((NH, NZ, 128), F32),
            dma((4,)),
            dma((CHUNKS,)),
            dma((CHUNKS,)),
            dma((2,)),
            dma((2,)),
            dma((2,)),
            dma((2,)),
            dma((CHUNKS,)),
            dma((CHUNKS,)),
            dma((3,)),
            dma((3,)),
        ],
        compiler_params=pltpu.CompilerParams(
            collective_id=0, has_side_effects=True, vmem_limit_bytes=56 * 1024 * 1024
        ),
        name="network",
    )(tensors.reshape(2, GROUP, 16, C), gates, closing_rows, closing_columns)


def solution(mesh):
    placed = (
        P(None, "sx", "sy", None, None),
        P(),
        P(None, ("sx", "sy"), None),
        P(None, ("sx", "sy"), None),
    )
    return jax.shard_map(local, mesh=mesh, in_specs=placed, out_specs=P(), check_vma=False)
```

time: 70.3 us -> 62.6 us (0.89)
  Pallas kernels: 68.1 us -> 61.1 us
  local copies, waits for them, and re-layouts: 2.12 us -> 1.38 us
    pallas_call x1, Pallas kernels: 68.1 us -> 61.1 us  [local(): pl.pallas_call(kernel, out_shape=jax.ShapeDtypeStruct((2, NZ * NH * NX *...]
    reshape x2 -> x0, local copies, waits for them, and re-layouts: 1.91 us -> none  [the longest x1 0.97 us: local(): out = out.reshape(2, 2, 2, NZ, 2, NX, AMP).transpose(4, 2, 3, 5, 0, 1, 6)]
    unnamed x0 -> x1, local copies, waits for them, and re-layouts: none -> 1.38 us
where the time goes in v3:
time: 62.6 us; the launch traced here: 62.4 us
  Pallas kernels  61.1 us (98%)
  local copies, waits for them, and re-layouts  1.38 us (2%)
    pallas_call x1, Pallas kernels, local(): pl.pallas_call(kernel, out_shape=jax.ShapeDtypeStruct((2, NZ * NH * NX *...  61.1 us
    unnamed x1, local copies, waits for them, and re-layouts  1.38 us

profile of v3, /device:TPU:1, one launch (start us, length us, event | category | flops | bytes accessed | tf_op | source)
XLA Modules:
  0.0 62.4 jit_solution(11753827303428155774)
XLA Ops:
  0.0 61.1 %network.1 = f32[2,4096]{1,0:T(2,128)} custom-call(bf16[2,64,16,256]{3,2,1,0:T(8,128)(2,1)} %bitcast.1, bf16[8,2,2,256,256]{4,3,2,1,0:T(8,128)(2,1)} %gates_ref.1, bf16[2,16,1024]{2,1,0:T(8,128)(2,1)} %rows_ref.1, f32[2,16,256]{2,1,0:T(8,128)} %cols_ref.1), custom_call_target="tpu_custom_call" | custom-call | tf_op jit(solution)/shard_map/network/pallas_call | solution.py:375
  61.1 1.4 %copy.6 = f32[2,4096]{1,0:T(2,128)} copy(f32[2,4096]{1,0:T(2,128)} %network.1) | data formatting | bytes 65536

commit v4 on v3

--- a/solution.py
+++ b/solution.py
@@ -184,7 +184,7 @@
     x_ref, gates_ref, rows_ref, cols_ref, out_ref,
     x_in, staged, recv, work1, work2, ret_send, ret, gates, right, tops, g_low, g_high, g_x,
     cols, crx, ccx, left, wbuf, finz, finx, finh,
-    local_sem, main_send, main_recv, small_send, small_recv, x_send, x_recv, back_send, back_recv, fin_send, fin_recv,
+    local_sem, main_send, main_recv, small_send, small_recv, x_send, x_recv, back_send, back_recv, fin_send, fin_recv, ready,
 ):
     mz, my, mx, mc = position()
     mh = bits_index(my, mc)
@@ -196,7 +196,6 @@
     y_peers = [lax.rem(my + d, NY) for d in range(NY)]
     c_peers = [lax.rem(mc + d, NC) for d in range(NC)]
     x_peers = [lax.rem(mx + d, NX) for d in range(NX)]
-    group = [(dz, dy, dc) for dz in Z_ORDER for dy in Y_ORDER for dc in range(NC) if dz or dy or dc]
     back = [(dy, dc) for dy in Y_ORDER for dc in range(NC) if dy or dc]
 
     x_copy = pltpu.make_async_copy(x_ref, x_in, local_sem.at[3])
@@ -209,10 +208,11 @@
     gates_copy.start()
 
     barrier = pltpu.get_barrier_semaphore()
-    for dz, dy, dc in group:
-        pl.semaphore_signal(barrier, inc=1, device_id=device(z_peers[dz], y_peers[dy], mx, c_peers[dc]), device_id_type=MESH)
-    for dx in range(1, NX):
-        pl.semaphore_signal(barrier, inc=1, device_id=device(mz, my, x_peers[dx], mc), device_id_type=MESH)
+    near = [(mz, y_peers[dy], mx, c_peers[dc]) for dy, dc in back]
+    near += [(z_peers[dz], my, mx, mc) for dz in (1, NZ - 1)]
+    near += [(mz, my, x_peers[dx], mc) for dx in range(1, NX)]
+    for there in near:
+        pl.semaphore_signal(barrier, inc=1, device_id=device(*there), device_id_type=MESH)
 
     cos, sin = unit(z0 + z1 + z2 + h_ones)
     low = lax.broadcasted_iota(jnp.int32, (2 * KR, C), 0) < KR
@@ -233,7 +233,7 @@
     lax.fori_loop(0, GROUP, stage, 0, unroll=4)
     for q in range(CHUNKS):
         recv[q, mine] = staged[q, mz * NH + mh]
-    pl.semaphore_wait(barrier, GROUP - 1 + NX - 1)
+    pl.semaphore_wait(barrier, len(near))
 
     def remote(src, dst, send, recv_sem, where):
         copy = pltpu.make_async_remote_copy(
@@ -241,17 +241,41 @@
         )
         copy.start()
 
-    for dz in Z_ORDER[:-1]:
+    def send_rows(dz):
         pz = z_peers[dz]
-        there = (pz, my, mx, mc)
         columns = pl.ds(pl.multiple_of(pz * 128, 128), 128)
-        remote(rows_ref.at[:, :, columns], crx.at[mx, mz], small_send.at[0], small_recv.at[0], there)
-        remote(ccx.at[mx, mz], ccx.at[mx, mz], small_send.at[1], small_recv.at[1], there)
-    for q in range(CHUNKS):
-        for dz, dy, dc in group:
-            pz, py, pc = z_peers[dz], y_peers[dy], c_peers[dc]
-            block = pz * NH + bits_index(py, pc)
-            remote(staged.at[q, block], recv.at[q, mine], main_send.at[q], main_recv.at[q], (pz, py, mx, pc))
+        remote(rows_ref.at[:, :, columns], crx.at[mx, mz], small_send.at[0], small_recv.at[0], (pz, my, mx, mc))
+
+    def send_columns(origin, dz, which):
+        slot = ccx.at[mx, z_peers[origin]]
+        remote(slot, slot, small_send.at[which], small_recv.at[which], (z_peers[dz], my, mx, mc))
+
+    def send_tensor(q, dz):
+        for dy in Y_ORDER:
+            for dc in range(NC):
+                if dz or dy or dc:
+                    pz, py, pc = z_peers[dz], y_peers[dy], c_peers[dc]
+                    block = pz * NH + bits_index(py, pc)
+                    remote(staged.at[q, block], recv.at[q, mine], main_send.at[q], main_recv.at[q], (pz, py, mx, pc))
+
+    send_tensor(0, 0)
+    for level in range(4):
+        pl.semaphore_signal(ready.at[level, 0], inc=1, device_id=device(z_peers[1], my, mx, mc), device_id_type=MESH)
+        pl.semaphore_signal(ready.at[level, 1], inc=1, device_id=device(z_peers[7], my, mx, mc), device_id_type=MESH)
+        distances = (level + 1, NZ - level - 1) if level < 3 else (4,)
+        for dz in distances:
+            send_rows(dz)
+            send_columns(0, dz, 1)
+        pl.semaphore_wait(ready.at[level, 0], 1)
+        pl.semaphore_wait(ready.at[level, 1], 1)
+        for dz in distances:
+            send_tensor(0, dz)
+    for dz in Z_ORDER:
+        send_tensor(1, dz)
+
+    for q in range(2, CHUNKS):
+        for dz in Z_ORDER:
+            send_tensor(q, dz)
 
     gates_copy.wait()
     triple_products(gates, 0, right, tops, g_low)
@@ -260,7 +284,7 @@
 
     own_rows.wait()
     wait_bytes(crx.at[0, pl.ds(0, NZ - 1)], small_recv.at[0])
-    wait_bytes(ccx.at[0, pl.ds(0, NZ - 1)], small_recv.at[1])
+    wait_bytes(ccx.at[0, pl.ds(0, 7)], small_recv.at[1])
     for dx in (2, 1, 3):
         there = (mz, my, x_peers[dx], mc)
         remote(crx.at[mx], crx.at[mx], x_send.at[0], x_recv.at[0], there)
@@ -302,7 +326,6 @@
                 if t & 2:
                     u = u * f1
                 total = u if total is None else total + u
-            total = total * 0.25
             re, neg = total[:, :C], total[:, C:]
             re, neg = cos * re + sin * neg, cos * neg - sin * re
             for z in range(NZ):
@@ -349,7 +372,7 @@
     for dz in Z_ORDER[:-1]:
         remote(finz.at[mz], finz.at[mz], fin_send.at[0], fin_recv.at[0], (z_peers[dz], my, mx, mc))
     wait_bytes(crx.at[0, pl.ds(0, NZ - 1)], small_send.at[0])
-    wait_bytes(ccx.at[0, pl.ds(0, NZ - 1)], small_send.at[1])
+    wait_bytes(ccx.at[0, pl.ds(0, 7)], small_send.at[1])
     wait_bytes(crx.at[pl.ds(0, NX - 1)], x_send.at[0])
     wait_bytes(ccx.at[pl.ds(0, NX - 1)], x_send.at[1])
     for q in range(CHUNKS):
@@ -372,7 +395,7 @@
 
 def local(tensors, gates, closing_rows, closing_columns):
     dma = pltpu.SemaphoreType.DMA
-    return pl.pallas_call(
+    out = pl.pallas_call(
         kernel,
         out_shape=jax.ShapeDtypeStruct((2, NZ * NH * NX * AMP), F32),
         in_specs=[pl.BlockSpec(memory_space=pl.ANY)] * 4,
@@ -402,20 +425,22 @@
             dma((4,)),
             dma((CHUNKS,)),
             dma((CHUNKS,)),
-            dma((2,)),
-            dma((2,)),
+            dma((3,)),
+            dma((3,)),
             dma((2,)),
             dma((2,)),
             dma((CHUNKS,)),
             dma((CHUNKS,)),
             dma((3,)),
             dma((3,)),
+            pltpu.SemaphoreType.REGULAR((4, 2)),
         ],
         compiler_params=pltpu.CompilerParams(
             collective_id=0, has_side_effects=True, vmem_limit_bytes=56 * 1024 * 1024
         ),
         name="network",
     )(tensors.reshape(2, GROUP, 16, C), gates, closing_rows, closing_columns)
+    return out * (1.0 / NX)
 
 
 def solution(mesh):

time: 62.6 us -> 61 us (0.974)
  Pallas kernels: 61.1 us -> 59.5 us
  other arithmetic: 0 us -> 1.39 us
  local copies, waits for them, and re-layouts: 1.38 us -> 0 us
    pallas_call x1, Pallas kernels: 61.1 us -> 59.5 us  [local(): pl.pallas_call(kernel, out_shape=jax.ShapeDtypeStruct((2, NZ * NH * NX *...]
    mul x0 -> x1, other arithmetic: none -> 1.39 us  [local(): return out * (1.0 / NX)]
    unnamed x1 -> x0, local copies, waits for them, and re-layouts: 1.38 us -> none
where the time goes in v4:
time: 61 us; the launch traced here: 60.9 us
  Pallas kernels  59.5 us (98%)
  other arithmetic  1.39 us (2%)
    pallas_call x1, Pallas kernels, local(): pl.pallas_call(kernel, out_shape=jax.ShapeDtypeStruct((2, NZ * NH * NX *...  59.5 us
    mul x1, other arithmetic, local(): return out * (1.0 / NX)  1.39 us

profile of v4, /device:TPU:1, one launch (start us, length us, event | category | flops | bytes accessed | tf_op | source)
XLA Modules:
  0.0 60.9 jit_solution(11001962999698328900)
XLA Ops:
  0.0 59.5 %network.1 = f32[2,4096]{1,0:T(2,128)} custom-call(bf16[2,64,16,256]{3,2,1,0:T(8,128)(2,1)} %bitcast.1, bf16[8,2,2,256,256]{4,3,2,1,0:T(8,128)(2,1)} %gates_ref.1, bf16[2,16,1024]{2,1,0:T(8,128)(2,1)} %rows_ref.1, f32[2,16,256]{2,1,0:T(8,128)} %cols_ref.1), custom_call_target="tpu_custom_call" | custom-call | tf_op jit(solution)/shard_map/network/pallas_call | solution.py:398
  59.5 1.4 %broadcast_multiply_fusion = f32[2,4096]{1,0:T(2,128)} fusion(f32[2,4096]{1,0:T(2,128)} %network.1), kind=kLoop, calls=%fused_computation | loop fusion | flops 8192 | bytes 65536 | tf_op jit(solution)/shard_map/mul | solution.py:443

commit v5 on v4

--- a/solution.py
+++ b/solution.py
@@ -196,6 +196,8 @@
     y_peers = [lax.rem(my + d, NY) for d in range(NY)]
     c_peers = [lax.rem(mc + d, NC) for d in range(NC)]
     x_peers = [lax.rem(mx + d, NX) for d in range(NX)]
+    crossing = [(dx, dy, dc) for dx in Y_ORDER for dy in Y_ORDER for dc in range(NC) if dx or dy or dc]
+    crossing.sort(key=lambda d: -min(d[0], 4 - d[0]) - min(d[1], 4 - d[1]))
     back = [(dy, dc) for dy in Y_ORDER for dc in range(NC) if dy or dc]
 
     x_copy = pltpu.make_async_copy(x_ref, x_in, local_sem.at[3])
@@ -379,18 +381,15 @@
         wait_bytes(recv.at[q, pl.ds(0, GROUP - 1)], main_send.at[q])
         wait_bytes(ret.at[q, pl.ds(0, NH - 1)], back_send.at[q])
     wait_bytes(finz.at[pl.ds(0, NZ - 1)], fin_recv.at[0])
-    finx[mx] = jnp.sum(finz[...], axis=0)
-    for dx in (2, 1, 3):
-        remote(finx.at[mx], finx.at[mx], fin_send.at[1], fin_recv.at[1], (mz, my, x_peers[dx], mc))
+    finx[mx * NH + mh] = jnp.sum(finz[...], axis=0)
+    for dx, dy, dc in crossing:
+        there = (mz, y_peers[dy], x_peers[dx], c_peers[dc])
+        remote(finx.at[mx * NH + mh], finx.at[mx * NH + mh], fin_send.at[1], fin_recv.at[1], there)
     wait_bytes(finz.at[pl.ds(0, NZ - 1)], fin_send.at[0])
-    wait_bytes(finx.at[pl.ds(0, NX - 1)], fin_recv.at[1])
-    finh[mh] = jnp.sum(finx[...], axis=0)
-    for dy, dc in back:
-        remote(finh.at[mh], finh.at[mh], fin_send.at[2], fin_recv.at[2], (mz, y_peers[dy], mx, c_peers[dc]))
-    wait_bytes(finx.at[pl.ds(0, NX - 1)], fin_send.at[1])
-    wait_bytes(finh.at[pl.ds(0, NH - 1)], fin_recv.at[2])
+    wait_bytes(finx.at[pl.ds(0, NX * NH - 1)], fin_recv.at[1])
+    finh[...] = jnp.sum(finx[...].reshape(NX, NH, NZ, 128), axis=0)
     assemble(finh, out_ref)
-    wait_bytes(finh.at[pl.ds(0, NH - 1)], fin_send.at[2])
+    wait_bytes(finx.at[pl.ds(0, NX * NH - 1)], fin_send.at[1])
 
 
 def local(tensors, gates, closing_rows, closing_columns):
@@ -420,7 +419,7 @@
             pltpu.VMEM((NZ, 128, C), BF16),
             pltpu.VMEM((NZ, NX * AMP, 2 * C), F32),
             pltpu.VMEM((NZ, NZ, 128), F32),
-            pltpu.VMEM((NX, NZ, 128), F32),
+            pltpu.VMEM((NX * NH, NZ, 128), F32),
             pltpu.VMEM((NH, NZ, 128), F32),
             dma((4,)),
             dma((CHUNKS,)),
@@ -431,8 +430,8 @@
             dma((2,)),
             dma((CHUNKS,)),
             dma((CHUNKS,)),
-            dma((3,)),
-            dma((3,)),
+            dma((2,)),
+            dma((2,)),
             pltpu.SemaphoreType.REGULAR((4, 2)),
         ],
         compiler_params=pltpu.CompilerParams(

time: 61 us -> 59 us (0.967)
  Pallas kernels: 59.5 us -> 57.5 us
    pallas_call x1, Pallas kernels: 59.5 us -> 57.5 us  [local(): pl.pallas_call(kernel, out_shape=jax.ShapeDtypeStruct((2, NZ * NH * NX *...]
where the time goes in v5:
time: 59 us; the launch traced here: 58.9 us
  Pallas kernels  57.5 us (97%)
  other arithmetic  1.39 us (2%)
    pallas_call x1, Pallas kernels, local(): pl.pallas_call(kernel, out_shape=jax.ShapeDtypeStruct((2, NZ * NH * NX *...  57.5 us
    mul x1, other arithmetic, local(): return out * (1.0 / NX)  1.39 us

profile of v5, /device:TPU:1, one launch (start us, length us, event | category | flops | bytes accessed | tf_op | source)
XLA Modules:
  0.0 58.9 jit_solution(5969378938411234970)
XLA Ops:
  0.0 57.5 %network.1 = f32[2,4096]{1,0:T(2,128)} custom-call(bf16[2,64,16,256]{3,2,1,0:T(8,128)(2,1)} %bitcast.1, bf16[8,2,2,256,256]{4,3,2,1,0:T(8,128)(2,1)} %gates_ref.1, bf16[2,16,1024]{2,1,0:T(8,128)(2,1)} %rows_ref.1, f32[2,16,256]{2,1,0:T(8,128)} %cols_ref.1), custom_call_target="tpu_custom_call" | custom-call | tf_op jit(solution)/shard_map/network/pallas_call | solution.py:397
  57.5 1.4 %broadcast_multiply_fusion = f32[2,4096]{1,0:T(2,128)} fusion(f32[2,4096]{1,0:T(2,128)} %network.1), kind=kLoop, calls=%fused_computation | loop fusion | flops 8192 | bytes 65536 | tf_op jit(solution)/shard_map/mul | solution.py:442

commit v6 on v5

--- a/solution.py
+++ b/solution.py
@@ -267,7 +267,14 @@
         distances = (level + 1, NZ - level - 1) if level < 3 else (4,)
         for dz in distances:
             send_rows(dz)
-            send_columns(0, dz, 1)
+            if level == 0:
+                send_columns(0, dz, 2)
+            if level == 1:
+                send_columns(0, dz, 1)
+        if level == 3:
+            wait_bytes(ccx.at[0, pl.ds(0, 2)], small_recv.at[1])
+            for origin, dz in ((6, 2), (6, 1), (2, 7)):
+                send_columns(origin, dz, 2)
         pl.semaphore_wait(ready.at[level, 0], 1)
         pl.semaphore_wait(ready.at[level, 1], 1)
         for dz in distances:
@@ -286,7 +293,7 @@
 
     own_rows.wait()
     wait_bytes(crx.at[0, pl.ds(0, NZ - 1)], small_recv.at[0])
-    wait_bytes(ccx.at[0, pl.ds(0, 7)], small_recv.at[1])
+    wait_bytes(ccx.at[0, pl.ds(0, 5)], small_recv.at[2])
     for dx in (2, 1, 3):
         there = (mz, my, x_peers[dx], mc)
         remote(crx.at[mx], crx.at[mx], x_send.at[0], x_recv.at[0], there)
@@ -343,11 +350,11 @@
             py, pc = y_peers[dy], c_peers[dc]
             remote(ret_send.at[q, bits_index(py, pc)], ret.at[q, mh], back_send.at[q], back_recv.at[q], (mz, py, mx, pc))
         ret[q, mh] = ret_send[q, mh]
-        if q == 0:
-            wait_bytes(crx.at[pl.ds(0, NX - 1)], x_recv.at[0])
-            wait_bytes(ccx.at[pl.ds(0, NX - 1)], x_recv.at[1])
-            closing_rows_in_order()
-            columns_through_x()
+
+    wait_bytes(crx.at[pl.ds(0, NX - 1)], x_recv.at[0])
+    wait_bytes(ccx.at[pl.ds(0, NX - 1)], x_recv.at[1])
+    closing_rows_in_order()
+    columns_through_x()
 
     for q in range(CHUNKS):
         wait_bytes(ret.at[q, pl.ds(0, NH - 1)], back_recv.at[q])
@@ -374,7 +381,8 @@
     for dz in Z_ORDER[:-1]:
         remote(finz.at[mz], finz.at[mz], fin_send.at[0], fin_recv.at[0], (z_peers[dz], my, mx, mc))
     wait_bytes(crx.at[0, pl.ds(0, NZ - 1)], small_send.at[0])
-    wait_bytes(ccx.at[0, pl.ds(0, 7)], small_send.at[1])
+    wait_bytes(ccx.at[0, pl.ds(0, 2)], small_send.at[1])
+    wait_bytes(ccx.at[0, pl.ds(0, 5)], small_send.at[2])
     wait_bytes(crx.at[pl.ds(0, NX - 1)], x_send.at[0])
     wait_bytes(ccx.at[pl.ds(0, NX - 1)], x_send.at[1])
     for q in range(CHUNKS):

time: 59 us -> 58.3 us (0.988)
  Pallas kernels: 57.5 us -> 56.8 us
    pallas_call x1, Pallas kernels: 57.5 us -> 56.8 us  [local(): pl.pallas_call(kernel, out_shape=jax.ShapeDtypeStruct((2, NZ * NH * NX *...]
where the time goes in v6:
time: 58.3 us; the launch traced here: 58.1 us
  Pallas kernels  56.8 us (97%)
  other arithmetic  1.39 us (2%)
    pallas_call x1, Pallas kernels, local(): pl.pallas_call(kernel, out_shape=jax.ShapeDtypeStruct((2, NZ * NH * NX *...  56.8 us
    mul x1, other arithmetic, local(): return out * (1.0 / NX)  1.39 us

profile of v6, /device:TPU:1, one launch (start us, length us, event | category | flops | bytes accessed | tf_op | source)
XLA Modules:
  0.0 58.1 jit_solution(17793856179166436800)
XLA Ops:
  0.0 56.8 %network.1 = f32[2,4096]{1,0:T(2,128)} custom-call(bf16[2,64,16,256]{3,2,1,0:T(8,128)(2,1)} %bitcast.1, bf16[8,2,2,256,256]{4,3,2,1,0:T(8,128)(2,1)} %gates_ref.1, bf16[2,16,1024]{2,1,0:T(8,128)(2,1)} %rows_ref.1, f32[2,16,256]{2,1,0:T(8,128)} %cols_ref.1), custom_call_target="tpu_custom_call" | custom-call | tf_op jit(solution)/shard_map/network/pallas_call | solution.py:405
  56.8 1.4 %broadcast_multiply_fusion = f32[2,4096]{1,0:T(2,128)} fusion(f32[2,4096]{1,0:T(2,128)} %network.1), kind=kLoop, calls=%fused_computation | loop fusion | flops 8192 | bytes 65536 | tf_op jit(solution)/shard_map/mul | solution.py:450

commit v7 on v6

--- a/solution.py
+++ b/solution.py
@@ -123,7 +123,7 @@
     return result
 
 
-def sections(q, recv, work1, work2, g_low, g_high, ret_send):
+def sections(q, recv, work1, work2, g_low, g_high, ret_send, send_back):
     def forward_z(h, carry):
         blocks = hadamard([recv[q, h * NZ + z].astype(F32) for z in range(NZ)])
         for t in range(NZ):
@@ -151,7 +151,9 @@
     lax.fori_loop(0, NH, forward_z, 0, unroll=UNROLL)
     lax.fori_loop(0, NZ, forward_h, 0, unroll=UNROLL)
     lax.fori_loop(0, NH, inverse_z, 0, unroll=UNROLL)
-    lax.fori_loop(0, NZ, inverse_h, 0, unroll=UNROLL)
+    for half in range(2):
+        lax.fori_loop(half * NZ // 2, (half + 1) * NZ // 2, inverse_h, 0, unroll=UNROLL)
+        send_back(half)
 
 
 def unit(turn):
@@ -345,10 +347,15 @@
 
     for q in range(CHUNKS):
         wait_bytes(recv.at[q, pl.ds(0, GROUP - 1)], main_recv.at[q])
-        sections(q, recv, work1, work2, g_low, g_high, ret_send)
-        for dy, dc in back:
-            py, pc = y_peers[dy], c_peers[dc]
-            remote(ret_send.at[q, bits_index(py, pc)], ret.at[q, mh], back_send.at[q], back_recv.at[q], (mz, py, mx, pc))
+
+        def send_back(half):
+            part = pl.ds(half * NZ // 2, NZ // 2)
+            for dy, dc in back:
+                py, pc = y_peers[dy], c_peers[dc]
+                source = ret_send.at[q, bits_index(py, pc), part]
+                remote(source, ret.at[q, mh, part], back_send.at[q], back_recv.at[q], (mz, py, mx, pc))
+
+        sections(q, recv, work1, work2, g_low, g_high, ret_send, send_back)
         ret[q, mh] = ret_send[q, mh]
 
     wait_bytes(crx.at[pl.ds(0, NX - 1)], x_recv.at[0])

time: 58.3 us -> 58.2 us (level)
  no operation moved by 1% of the time
where the time goes in v7:
time: 58.2 us; the launch traced here: 58.1 us
  Pallas kernels  56.7 us (97%)
  other arithmetic  1.39 us (2%)
    pallas_call x1, Pallas kernels, local(): pl.pallas_call(kernel, out_shape=jax.ShapeDtypeStruct((2, NZ * NH * NX *...  56.7 us
    mul x1, other arithmetic, local(): return out * (1.0 / NX)  1.39 us

profile of v7, /device:TPU:1, one launch (start us, length us, event | category | flops | bytes accessed | tf_op | source)
XLA Modules:
  0.0 58.1 jit_solution(8158780934649657837)
XLA Ops:
  0.0 56.7 %network.1 = f32[2,4096]{1,0:T(2,128)} custom-call(bf16[2,64,16,256]{3,2,1,0:T(8,128)(2,1)} %bitcast.1, bf16[8,2,2,256,256]{4,3,2,1,0:T(8,128)(2,1)} %gates_ref.1, bf16[2,16,1024]{2,1,0:T(8,128)(2,1)} %rows_ref.1, f32[2,16,256]{2,1,0:T(8,128)} %cols_ref.1), custom_call_target="tpu_custom_call" | custom-call | tf_op jit(solution)/shard_map/network/pallas_call | solution.py:412
  56.7 1.4 %broadcast_multiply_fusion = f32[2,4096]{1,0:T(2,128)} fusion(f32[2,4096]{1,0:T(2,128)} %network.1), kind=kLoop, calls=%fused_computation | loop fusion | flops 8192 | bytes 65536 | tf_op jit(solution)/shard_map/mul | solution.py:457
